TPU v7x, 32 devices: a whole 2x2x4 slice. The times are simulated.
32 devices in a mesh: tm: 8 (over y, x, core), space: 4 (over z).
Axes of the slice: x: 2, y: 2, z: 4, core: 2. Of those that a mesh axis runs over, the one named last changes fastest.
Arguments:
- gauge_links: float32 [8, 2, 3, 3, 3, 8, 1024], P('tm', None, None, None, None, 'space'), may hold values from -1 to 1, as said below
- time_links: float32 [8, 2, 3, 3, 8, 1024], P('tm', None, None, None, 'space'), may hold values from -1 to 1, as said below
- sink_vectors: bfloat16 [8, 2, 128, 3, 8, 1024], P('tm', None, None, None, 'space'), may hold values from -0.29882812 to 0.29882812
- source_times: int32 [4], replicated, may hold values from 0 to 7
- source_index: int32 [4, 2], replicated, may hold values from 0 to 127
- kinetic_coef: float32 [4, 2], replicated, may hold values from 0.005 to 0.12
Outputs:
- perambulator: float32 [2, 4, 2, 8, 128], P(None, None, None, 'tm', 'space')
Inputs may be any that keep to these rules, and one draw needn't show every extreme that they name: `gauge_links`: each link is a special unitary 3 x 3 matrix. `time_links`: each link is a special unitary 3 x 3 matrix.
All inputs are finite; a program needn't handle non-finite values.
Results may differ from a plain program's by a relative error of at most 0.0029.
Values may be sent and summed in bfloat16 or wider, within the bound.
A program may use at most 128 MiB of HBM per device.

v0:
```python
import jax
import jax.numpy as jnp
from jax import lax
from jax.sharding import PartitionSpec as P

LS = 32


def padded(block, sides, width):
    for axis, dim in sides:
        count = lax.axis_size(axis)
        forward = [(i, i + 1) for i in range(count - 1)]
        forward.append((count - 1, 0))
        backward = [(target, source) for source, target in forward]
        low = lax.ppermute(
            lax.slice_in_dim(block, block.shape[dim] - width, None, axis=dim), axis, forward
        )
        high = lax.ppermute(lax.slice_in_dim(block, 0, width, axis=dim), axis, backward)
        block = jnp.concatenate([low, block, high], axis=dim)
    return block


def shifted(x, axis, by):
    length = lax.axis_size(axis)
    return lax.ppermute(x, axis, [(i, (i + by) % length) for i in range(length)])


def colour_apply(matrix, vector_in):
    real_rows = []
    imag_rows = []
    for out_colour in range(3):
        real_sum = (
            matrix[0, out_colour, 0] * vector_in[0, 0] - matrix[1, out_colour, 0] * vector_in[1, 0]
        )
        imag_sum = (
            matrix[0, out_colour, 0] * vector_in[1, 0] + matrix[1, out_colour, 0] * vector_in[0, 0]
        )
        for in_colour in (1, 2):
            real_sum = (
                real_sum
                + matrix[0, out_colour, in_colour] * vector_in[0, in_colour]
                - matrix[1, out_colour, in_colour] * vector_in[1, in_colour]
            )
            imag_sum = (
                imag_sum
                + matrix[0, out_colour, in_colour] * vector_in[1, in_colour]
                + matrix[1, out_colour, in_colour] * vector_in[0, in_colour]
            )
        real_rows.append(real_sum)
        imag_rows.append(imag_sum)
    return jnp.stack([jnp.stack(real_rows), jnp.stack(imag_rows)])


def colour_adjoint(matrix, vector_in):
    real_rows = []
    imag_rows = []
    for out_colour in range(3):
        real_sum = (
            matrix[0, 0, out_colour] * vector_in[0, 0] + matrix[1, 0, out_colour] * vector_in[1, 0]
        )
        imag_sum = (
            matrix[0, 0, out_colour] * vector_in[1, 0] - matrix[1, 0, out_colour] * vector_in[0, 0]
        )
        for in_colour in (1, 2):
            real_sum = (
                real_sum
                + matrix[0, in_colour, out_colour] * vector_in[0, in_colour]
                + matrix[1, in_colour, out_colour] * vector_in[1, in_colour]
            )
            imag_sum = (
                imag_sum
                + matrix[0, in_colour, out_colour] * vector_in[1, in_colour]
                - matrix[1, in_colour, out_colour] * vector_in[0, in_colour]
            )
        real_rows.append(real_sum)
        imag_rows.append(imag_sum)
    return jnp.stack([jnp.stack(real_rows), jnp.stack(imag_rows)])


def shift_up(values, direction):
    if direction == 1:
        return jnp.roll(values, -LS, axis=-1)
    z_index = jnp.arange(values.shape[-1]) % LS
    return jnp.where(
        z_index == LS - 1, jnp.roll(values, LS - 1, axis=-1), jnp.roll(values, -1, axis=-1)
    )


def shift_down(values, direction):
    if direction == 1:
        return jnp.roll(values, LS, axis=-1)
    z_index = jnp.arange(values.shape[-1]) % LS
    return jnp.where(
        z_index == 0, jnp.roll(values, -(LS - 1), axis=-1), jnp.roll(values, 1, axis=-1)
    )


def laplace(widened, field_offset, links, link_offset, lower, upper):
    centre = widened[:, :, :, lower + field_offset : upper + field_offset]
    summed = -6.0 * centre
    x_links = links[:, 0]
    summed = summed + colour_apply(
        x_links[:, :, :, :, lower + link_offset : upper + link_offset],
        widened[:, :, :, lower + 1 + field_offset : upper + 1 + field_offset],
    )
    summed = summed + colour_adjoint(
        x_links[:, :, :, :, lower - 1 + link_offset : upper - 1 + link_offset],
        widened[:, :, :, lower - 1 + field_offset : upper - 1 + field_offset],
    )
    for direction in (1, 2):
        matrix = links[:, direction][:, :, :, :, lower + link_offset : upper + link_offset]
        summed = summed + colour_apply(matrix, shift_up(centre, direction))
        summed = summed + colour_adjoint(
            shift_down(matrix, direction), shift_down(centre, direction)
        )
    return summed


def field_rims(wavefn):
    return padded(wavefn, (("space", 3),), 1)


def project(sinks, rounded):
    real_part = jnp.einsum(
        "ecxs,cvxs->ve", sinks[0], rounded[0], preferred_element_type=jnp.float32
    ) + jnp.einsum("ecxs,cvxs->ve", sinks[1], rounded[1], preferred_element_type=jnp.float32)
    imag_part = jnp.einsum(
        "ecxs,cvxs->ve", sinks[0], rounded[1], preferred_element_type=jnp.float32
    ) - jnp.einsum("ecxs,cvxs->ve", sinks[1], rounded[0], preferred_element_type=jnp.float32)
    return jnp.stack([real_part, imag_part])


def local(gauge_links, time_links, sink_vectors, source_times, source_index, kinetic_coef):
    planes = gauge_links.shape[5]
    n_time = lax.axis_size("tm")
    my_time = lax.axis_index("tm")
    groups = kinetic_coef.shape[0]
    per_group = kinetic_coef.shape[1]
    start_flat = jnp.repeat(source_times, per_group)
    index_flat = source_index.reshape(-1)
    coef_flat = kinetic_coef.reshape(-1)
    my_sinks = sink_vectors[0]
    source = jnp.take(my_sinks, index_flat, axis=1).astype(jnp.float32).transpose(0, 2, 1, 3, 4)
    is_source = (start_flat == my_time)[None, None, :, None, None]

    def advance(wavefn, links, temporal, weight):
        halfway = wavefn + weight * laplace(field_rims(wavefn), 1, links, 1, 0, planes)
        turned = colour_adjoint(temporal[:, :, :, :, 1 : planes + 1], halfway)
        return turned + weight * laplace(field_rims(turned), 1, links, 1, 0, planes)

    time_part = time_links[:, :, None]
    below = shifted(
        gauge_links[:, :, 0:1, :, :, planes - 1 : planes].astype(jnp.bfloat16), "space", 1
    ).astype(jnp.float32)
    blank = jnp.zeros_like(gauge_links[:, :, 1:, :, :, 0:1])
    gauge_wide = jnp.concatenate([jnp.concatenate([below, blank], axis=2), gauge_links], axis=5)
    time_wide = jnp.concatenate([jnp.zeros_like(time_part[:, :, :, :, :, 0:1]), time_part], axis=5)
    links = jnp.moveaxis(gauge_wide, 0, 4)
    temporal = jnp.moveaxis(time_wide[:, :, 0], 0, 3)
    weight = (0.5 * coef_flat)[None, None, :, None, None]
    needed = ((my_time - start_flat) % n_time)[None, None, :, None, None]

    def one_round(rounds, state_pair):
        wavefn, recorded = state_pair
        entering = jnp.where(is_source, source, wavefn)
        evolved = advance(entering, links, temporal, weight)
        recorded = jnp.where(needed == rounds, evolved, recorded)
        return (evolved, recorded)

    def loop_round(rounds, state_pair):
        evolved, recorded = one_round(rounds, state_pair)
        return (shifted(evolved, "tm", 1), recorded)

    empty = jnp.zeros_like(source)
    state_pair = lax.fori_loop(0, n_time - 1, loop_round, (empty, empty))
    _, recorded = one_round(n_time - 1, state_pair)
    correlations = project(my_sinks, recorded.astype(jnp.bfloat16))
    correlations = correlations.reshape(2, groups, per_group, 1, my_sinks.shape[1])
    return lax.psum_scatter(correlations, "space", scatter_dimension=4, tiled=True)


def solution(mesh):
    placed = (
        P("tm", None, None, None, None, "space", None),
        P("tm", None, None, None, "space", None),
        P("tm", None, None, None, "space", None),
        P(),
        P(),
        P(),
    )
    return jax.shard_map(
        local,
        mesh=mesh,
        in_specs=placed,
        out_specs=P(None, None, None, "tm", "space"),
        check_vma=False,
    )
```

profile of v0, /device:TPU:0, one launch (start us, length us, event | category | flops | bytes accessed | tf_op | source)
XLA Modules:
  0.0 554.9 jit_solution(3297556827526303536)
XLA Ops:
  7.6 3.1 collective-permute-start.5
  16.8 5.3 fusion.357
  22.1 2.9 gather_fusion
  32.8 459.7 %while.18 = (s32[]{:T(128)}, f32[2,3,8,2,1024]{4,3,2,1,0:T(2,128)S(1)}, bf16[2,3,8,2,1024]{4,3,2,1,0:T(2,128)(2,1)S(1)}, f32[2,3,3,1,3,1024]{5,4,3,2,1,0:T(4,128...) while((s32[]{:T(128)}, ...), condition=%wide.region_1.2_spmd.clone, body=%wide.region_0.1_spmd.clone.sunk | while | flops 24496228 | bytes 82878080 | solution.py:175
  52.7 2.1 collective-permute-start.1
  66.5 2.1 maximum_select_fusion.11
  90.5 3.9 collective-permute-start.3
  95.2 4.5 collective-permute-done.3
  100.8 2.1 collective-permute-done.2
  105.4 8.1 %collective-permute-done.4 = f32[2,3,8,2,1024]{4,3,2,1,0:T(2,128)S(1)} collective-permute-done((f32[2,3,8,2,1024]{4,3,2,1,0:T(2,128)S(1)}, f32[2,3,8,2,1024]{4,3,2,1,0:T(2,128)S(1)}, u32[]{:S(2)}, u32[]{:S(2)}) %collective-permute-start.4) | collective-permute-done | bytes 393248 | tf_op jit(solution)/shard_map/while/body/eval_jaxpr/ppermute | solution.py:25
  115.6 2.2 collective-permute-start.1
  129.6 2.1 maximum_select_fusion.11
  153.5 3.9 collective-permute-start.3
  158.2 3.5 collective-permute-done.3
  162.9 2.4 collective-permute-done.2
  167.7 8.1 %collective-permute-done.4 = f32[2,3,8,2,1024]{4,3,2,1,0:T(2,128)S(1)} collective-permute-done((f32[2,3,8,2,1024]{4,3,2,1,0:T(2,128)S(1)}, f32[2,3,8,2,1024]{4,3,2,1,0:T(2,128)S(1)}, u32[]{:S(2)}, u32[]{:S(2)}) %collective-permute-start.4) | collective-permute-done | bytes 393248 | tf_op jit(solution)/shard_map/while/body/eval_jaxpr/ppermute | solution.py:25
  177.9 2.0 collective-permute-start.1
  191.7 2.1 maximum_select_fusion.11
  215.7 3.8 collective-permute-start.3
  220.3 3.2 collective-permute-done.3
  224.7 2.7 collective-permute-done.2
  229.8 8.1 %collective-permute-done.4 = f32[2,3,8,2,1024]{4,3,2,1,0:T(2,128)S(1)} collective-permute-done((f32[2,3,8,2,1024]{4,3,2,1,0:T(2,128)S(1)}, f32[2,3,8,2,1024]{4,3,2,1,0:T(2,128)S(1)}, u32[]{:S(2)}, u32[]{:S(2)}) %collective-permute-start.4) | collective-permute-done | bytes 393248 | tf_op jit(solution)/shard_map/while/body/eval_jaxpr/ppermute | solution.py:25
  253.8 2.1 maximum_select_fusion.11
  277.8 3.6 collective-permute-start.3
  282.2 3.3 collective-permute-done.3
  286.7 2.6 collective-permute-done.2
  291.7 8.1 %collective-permute-done.4 = f32[2,3,8,2,1024]{4,3,2,1,0:T(2,128)S(1)} collective-permute-done((f32[2,3,8,2,1024]{4,3,2,1,0:T(2,128)S(1)}, f32[2,3,8,2,1024]{4,3,2,1,0:T(2,128)S(1)}, u32[]{:S(2)}, u32[]{:S(2)}) %collective-permute-start.4) | collective-permute-done | bytes 393248 | tf_op jit(solution)/shard_map/while/body/eval_jaxpr/ppermute | solution.py:25
  301.9 1.8 collective-permute-start.1
  315.7 2.1 maximum_select_fusion.11
  339.6 3.7 collective-permute-start.3
  344.1 3.0 collective-permute-done.3
  348.3 2.5 collective-permute-done.2
  353.2 8.1 %collective-permute-done.4 = f32[2,3,8,2,1024]{4,3,2,1,0:T(2,128)S(1)} collective-permute-done((f32[2,3,8,2,1024]{4,3,2,1,0:T(2,128)S(1)}, f32[2,3,8,2,1024]{4,3,2,1,0:T(2,128)S(1)}, u32[]{:S(2)}, u32[]{:S(2)}) %collective-permute-start.4) | collective-permute-done | bytes 393248 | tf_op jit(solution)/shard_map/while/body/eval_jaxpr/ppermute | solution.py:25
  377.3 2.1 maximum_select_fusion.11
  401.2 3.2 collective-permute-start.3
  405.2 3.1 collective-permute-done.3
  409.5 2.8 collective-permute-done.2
  414.7 8.1 %collective-permute-done.4 = f32[2,3,8,2,1024]{4,3,2,1,0:T(2,128)S(1)} collective-permute-done((f32[2,3,8,2,1024]{4,3,2,1,0:T(2,128)S(1)}, f32[2,3,8,2,1024]{4,3,2,1,0:T(2,128)S(1)}, u32[]{:S(2)}, u32[]{:S(2)}) %collective-permute-start.4) | collective-permute-done | bytes 393248 | tf_op jit(solution)/shard_map/while/body/eval_jaxpr/ppermute | solution.py:25
  438.7 2.1 maximum_select_fusion.11
  462.7 3.4 collective-permute-start.3
  466.9 3.2 collective-permute-done.3
  471.3 2.7 collective-permute-done.2
  476.4 8.1 %collective-permute-done.4 = f32[2,3,8,2,1024]{4,3,2,1,0:T(2,128)S(1)} collective-permute-done((f32[2,3,8,2,1024]{4,3,2,1,0:T(2,128)S(1)}, f32[2,3,8,2,1024]{4,3,2,1,0:T(2,128)S(1)}, u32[]{:S(2)}, u32[]{:S(2)}) %collective-permute-start.4) | collective-permute-done | bytes 393248 | tf_op jit(solution)/shard_map/while/body/eval_jaxpr/ppermute | solution.py:25
  496.5 3.2 collective-permute-start.6
  501.7 2.2 collective-permute-done.7
  510.1 3.5 collective-permute-start.8
  513.8 5.6 %collective-permute-done.9 = f32[2,3,8,1,1024]{4,2,3,1,0:T(8,128)S(1)} collective-permute-done((f32[2,3,8,1,1024]{4,2,3,1,0:T(8,128)S(1)}, f32[2,3,8,1,1024]{4,2,3,1,0:T(8,128)S(1)}, u32[]{:S(2)}, u32[]{:S(2)}) %collective-permute-start.9) | collective-permute-done | bytes 196640 | tf_op jit(solution)/shard_map/ppermute | solution.py:15
  528.5 17.4 %reduce-scatter.4.cloned.1.call-done = f32[32,16]{1,0:T(8,128)} async-done(((f32[128,16]{1,0:T(8,128)}), f32[32,16]{1,0:T(8,128)}) %reduce-scatter.4.cloned.1.call-update) | async-done | bytes 2064
  (3345 shorter events, 302.6 us)
Async XLA Ops:
  6.5 539.4 %reduce-scatter.4.cloned.1.call-start = ((), (), s32[]{:S(2)}) async-start(), calls=%async_computation.1 | async-start | bytes 81920
  7.6 21.7 %collective-permute-start.5 = (bf16[1,2,1,3,3,1,1024]{6,5,4,3,1,2,0:T(2,128)(2,1)S(1)}, bf16[1,2,1,3,3,1,1024]{6,5,4,3,1,2,0:T(2,128)(2,1)S(1)}, u32[]{:S(2)}, u32[]{:S(2)}) collective-permute-start(bf16[1,2,1,3,3,1,1024]{6,5,4,3,1,2,0:T(2,128)(2,1)S(1)} %copy.83), channel_id=1, source_target_pairs={{0,1},{1,2},{2,3},{3,0},{4,5},{5,6},{6,7},{7,4},{8,9},{9,10},{10,1... | collective-permute-start | bytes 110600 | tf_op jit(solution)/shard_map/ppermute | solution.py:25
  10.7 20.7 %copy-start.170 = (pred[1024]{0:T(1024)(128)(4,1)}, pred[1024]{0:T(1024)(128)(4,1)S(1)}, u32[]{:S(2)}) copy-start(pred[1024]{0:T(1024)(128)(4,1)S(1)} %fusion.308) | copy-start | bytes 3076
  13.5 11.4 %copy-start.174 = (pred[8]{0:T(512)(128)(4,1)}, pred[8]{0:T(512)(128)(4,1)S(1)}, u32[]{:S(2)}) copy-start(pred[8]{0:T(512)(128)(4,1)S(1)} %compare_and_fusion) | copy-start | bytes 28
  52.7 22.8 %collective-permute-start.1 = (f32[2,3,8,1,1024]{4,3,2,1,0:T(1,128)}, f32[2,3,8,1,1024]{4,3,2,1,0:T(1,128)}, u32[]{:S(2)}, u32[]{:S(2)}) collective-permute-start(f32[2,3,8,1,1024]{4,3,2,1,0:T(1,128)} %get-tuple-element.1466), channel_id=1, source_target_pairs={{1,0},{2,1},{3,2},{0,3},{5,4},{6,5},{7,6},{4,7},{9,8},{10,9},{11,1... | collective-permute-start | bytes 589832 | tf_op jit(solution)/shard_map/while/body/eval_jaxpr/ppermute | solution.py:18
  54.8 23.2 %collective-permute-start = (f32[2,3,8,1,1024]{4,3,2,1,0:T(1,128)}, f32[2,3,8,1,1024]{4,3,2,1,0:T(1,128)}, u32[]{:S(2)}, u32[]{:S(2)}) collective-permute-start(f32[2,3,8,1,1024]{4,3,2,1,0:T(1,128)} %get-tuple-element.1433), channel_id=1, source_target_pairs={{0,1},{1,2},{2,3},{3,0},{4,5},{5,6},{6,7},{7,4},{8,9},{9,10},{10,1... | collective-permute-start | bytes 589832 | tf_op jit(solution)/shard_map/while/body/eval_jaxpr/ppermute | solution.py:15
  90.5 9.2 %collective-permute-start.3 = (f32[2,3,8,1,1024]{4,3,2,1,0:T(1,128)S(1)}, f32[2,3,8,1,1024]{4,3,2,1,0:T(1,128)S(1)}, u32[]{:S(2)}, u32[]{:S(2)}) collective-permute-start(f32[2,3,8,1,1024]{4,3,2,1,0:T(1,128)S(1)} %get-tuple-element.1562), channel_id=1, source_target_pairs={{1,0},{2,1},{3,2},{0,3},{5,4},{6,5},{7,6},{4,7},{9,8},{10,9},{11,1... | collective-permute-start | bytes 589832 | tf_op jit(solution)/shard_map/while/body/eval_jaxpr/ppermute | solution.py:18
  94.4 8.6 %collective-permute-start.2 = (f32[2,3,8,1,1024]{4,3,2,1,0:T(1,128)S(1)}, f32[2,3,8,1,1024]{4,3,2,1,0:T(1,128)S(1)}, u32[]{:S(2)}, u32[]{:S(2)}) collective-permute-start(f32[2,3,8,1,1024]{4,3,2,1,0:T(1,128)S(1)} %get-tuple-element.1549), channel_id=1, source_target_pairs={{0,1},{1,2},{2,3},{3,0},{4,5},{5,6},{6,7},{7,4},{8,9},{9,10},{10,1... | collective-permute-start | bytes 589832 | tf_op jit(solution)/shard_map/while/body/eval_jaxpr/ppermute | solution.py:15
  104.0 9.4 %copy-start.3 = (f32[2,3,8,2,1024]{4,3,2,1,0:T(2,128)S(1)}, f32[2,3,8,2,1024]{4,3,2,1,0:T(2,128)}, u32[]{:S(2)}) copy-start(f32[2,3,8,2,1024]{4,3,2,1,0:T(2,128)} %copy-done.2) | copy-start | bytes 1179652 | tf_op jit(solution)/shard_map/while
  105.3 8.2 %collective-permute-start.4 = (f32[2,3,8,2,1024]{4,3,2,1,0:T(2,128)S(1)}, f32[2,3,8,2,1024]{4,3,2,1,0:T(2,128)S(1)}, u32[]{:S(2)}, u32[]{:S(2)}) collective-permute-start(f32[2,3,8,2,1024]{4,3,2,1,0:T(2,128)S(1)} %get-tuple-element.1575), channel_id=1, source_target_pairs={{0,4},{4,8},{8,12},{12,16},{16,20},{20,24},{24,28},{28,0},{1,5},{5... | collective-permute-start | bytes 1179656 | tf_op jit(solution)/shard_map/while/body/eval_jaxpr/ppermute | solution.py:25
  115.6 23.0 %collective-permute-start.1 = (f32[2,3,8,1,1024]{4,3,2,1,0:T(1,128)}, f32[2,3,8,1,1024]{4,3,2,1,0:T(1,128)}, u32[]{:S(2)}, u32[]{:S(2)}) collective-permute-start(f32[2,3,8,1,1024]{4,3,2,1,0:T(1,128)} %get-tuple-element.1466), channel_id=1, source_target_pairs={{1,0},{2,1},{3,2},{0,3},{5,4},{6,5},{7,6},{4,7},{9,8},{10,9},{11,1... | collective-permute-start | bytes 589832 | tf_op jit(solution)/shard_map/while/body/eval_jaxpr/ppermute | solution.py:18
  117.8 23.2 %collective-permute-start = (f32[2,3,8,1,1024]{4,3,2,1,0:T(1,128)}, f32[2,3,8,1,1024]{4,3,2,1,0:T(1,128)}, u32[]{:S(2)}, u32[]{:S(2)}) collective-permute-start(f32[2,3,8,1,1024]{4,3,2,1,0:T(1,128)} %get-tuple-element.1433), channel_id=1, source_target_pairs={{0,1},{1,2},{2,3},{3,0},{4,5},{5,6},{6,7},{7,4},{8,9},{9,10},{10,1... | collective-permute-start | bytes 589832 | tf_op jit(solution)/shard_map/while/body/eval_jaxpr/ppermute | solution.py:15
  153.5 8.2 %collective-permute-start.3 = (f32[2,3,8,1,1024]{4,3,2,1,0:T(1,128)S(1)}, f32[2,3,8,1,1024]{4,3,2,1,0:T(1,128)S(1)}, u32[]{:S(2)}, u32[]{:S(2)}) collective-permute-start(f32[2,3,8,1,1024]{4,3,2,1,0:T(1,128)S(1)} %get-tuple-element.1562), channel_id=1, source_target_pairs={{1,0},{2,1},{3,2},{0,3},{5,4},{6,5},{7,6},{4,7},{9,8},{10,9},{11,1... | collective-permute-start | bytes 589832 | tf_op jit(solution)/shard_map/while/body/eval_jaxpr/ppermute | solution.py:18
  157.4 7.9 %collective-permute-start.2 = (f32[2,3,8,1,1024]{4,3,2,1,0:T(1,128)S(1)}, f32[2,3,8,1,1024]{4,3,2,1,0:T(1,128)S(1)}, u32[]{:S(2)}, u32[]{:S(2)}) collective-permute-start(f32[2,3,8,1,1024]{4,3,2,1,0:T(1,128)S(1)} %get-tuple-element.1549), channel_id=1, source_target_pairs={{0,1},{1,2},{2,3},{3,0},{4,5},{5,6},{6,7},{7,4},{8,9},{9,10},{10,1... | collective-permute-start | bytes 589832 | tf_op jit(solution)/shard_map/while/body/eval_jaxpr/ppermute | solution.py:15
  166.3 9.4 %copy-start.3 = (f32[2,3,8,2,1024]{4,3,2,1,0:T(2,128)S(1)}, f32[2,3,8,2,1024]{4,3,2,1,0:T(2,128)}, u32[]{:S(2)}) copy-start(f32[2,3,8,2,1024]{4,3,2,1,0:T(2,128)} %copy-done.2) | copy-start | bytes 1179652 | tf_op jit(solution)/shard_map/while
  167.6 8.2 %collective-permute-start.4 = (f32[2,3,8,2,1024]{4,3,2,1,0:T(2,128)S(1)}, f32[2,3,8,2,1024]{4,3,2,1,0:T(2,128)S(1)}, u32[]{:S(2)}, u32[]{:S(2)}) collective-permute-start(f32[2,3,8,2,1024]{4,3,2,1,0:T(2,128)S(1)} %get-tuple-element.1575), channel_id=1, source_target_pairs={{0,4},{4,8},{8,12},{12,16},{16,20},{20,24},{24,28},{28,0},{1,5},{5... | collective-permute-start | bytes 1179656 | tf_op jit(solution)/shard_map/while/body/eval_jaxpr/ppermute | solution.py:25
  177.9 22.8 %collective-permute-start.1 = (f32[2,3,8,1,1024]{4,3,2,1,0:T(1,128)}, f32[2,3,8,1,1024]{4,3,2,1,0:T(1,128)}, u32[]{:S(2)}, u32[]{:S(2)}) collective-permute-start(f32[2,3,8,1,1024]{4,3,2,1,0:T(1,128)} %get-tuple-element.1466), channel_id=1, source_target_pairs={{1,0},{2,1},{3,2},{0,3},{5,4},{6,5},{7,6},{4,7},{9,8},{10,9},{11,1... | collective-permute-start | bytes 589832 | tf_op jit(solution)/shard_map/while/body/eval_jaxpr/ppermute | solution.py:18
  179.9 23.2 %collective-permute-start = (f32[2,3,8,1,1024]{4,3,2,1,0:T(1,128)}, f32[2,3,8,1,1024]{4,3,2,1,0:T(1,128)}, u32[]{:S(2)}, u32[]{:S(2)}) collective-permute-start(f32[2,3,8,1,1024]{4,3,2,1,0:T(1,128)} %get-tuple-element.1433), channel_id=1, source_target_pairs={{0,1},{1,2},{2,3},{3,0},{4,5},{5,6},{6,7},{7,4},{8,9},{9,10},{10,1... | collective-permute-start | bytes 589832 | tf_op jit(solution)/shard_map/while/body/eval_jaxpr/ppermute | solution.py:15
  215.7 7.9 %collective-permute-start.3 = (f32[2,3,8,1,1024]{4,3,2,1,0:T(1,128)S(1)}, f32[2,3,8,1,1024]{4,3,2,1,0:T(1,128)S(1)}, u32[]{:S(2)}, u32[]{:S(2)}) collective-permute-start(f32[2,3,8,1,1024]{4,3,2,1,0:T(1,128)S(1)} %get-tuple-element.1562), channel_id=1, source_target_pairs={{1,0},{2,1},{3,2},{0,3},{5,4},{6,5},{7,6},{4,7},{9,8},{10,9},{11,1... | collective-permute-start | bytes 589832 | tf_op jit(solution)/shard_map/while/body/eval_jaxpr/ppermute | solution.py:18
  219.5 7.9 %collective-permute-start.2 = (f32[2,3,8,1,1024]{4,3,2,1,0:T(1,128)S(1)}, f32[2,3,8,1,1024]{4,3,2,1,0:T(1,128)S(1)}, u32[]{:S(2)}, u32[]{:S(2)}) collective-permute-start(f32[2,3,8,1,1024]{4,3,2,1,0:T(1,128)S(1)} %get-tuple-element.1549), channel_id=1, source_target_pairs={{0,1},{1,2},{2,3},{3,0},{4,5},{5,6},{6,7},{7,4},{8,9},{9,10},{10,1... | collective-permute-start | bytes 589832 | tf_op jit(solution)/shard_map/while/body/eval_jaxpr/ppermute | solution.py:15
  228.5 9.4 %copy-start.3 = (f32[2,3,8,2,1024]{4,3,2,1,0:T(2,128)S(1)}, f32[2,3,8,2,1024]{4,3,2,1,0:T(2,128)}, u32[]{:S(2)}) copy-start(f32[2,3,8,2,1024]{4,3,2,1,0:T(2,128)} %copy-done.2) | copy-start | bytes 1179652 | tf_op jit(solution)/shard_map/while
  229.8 8.2 %collective-permute-start.4 = (f32[2,3,8,2,1024]{4,3,2,1,0:T(2,128)S(1)}, f32[2,3,8,2,1024]{4,3,2,1,0:T(2,128)S(1)}, u32[]{:S(2)}, u32[]{:S(2)}) collective-permute-start(f32[2,3,8,2,1024]{4,3,2,1,0:T(2,128)S(1)} %get-tuple-element.1575), channel_id=1, source_target_pairs={{0,4},{4,8},{8,12},{12,16},{16,20},{20,24},{24,28},{28,0},{1,5},{5... | collective-permute-start | bytes 1179656 | tf_op jit(solution)/shard_map/while/body/eval_jaxpr/ppermute | solution.py:25
  240.1 22.8 %collective-permute-start.1 = (f32[2,3,8,1,1024]{4,3,2,1,0:T(1,128)}, f32[2,3,8,1,1024]{4,3,2,1,0:T(1,128)}, u32[]{:S(2)}, u32[]{:S(2)}) collective-permute-start(f32[2,3,8,1,1024]{4,3,2,1,0:T(1,128)} %get-tuple-element.1466), channel_id=1, source_target_pairs={{1,0},{2,1},{3,2},{0,3},{5,4},{6,5},{7,6},{4,7},{9,8},{10,9},{11,1... | collective-permute-start | bytes 589832 | tf_op jit(solution)/shard_map/while/body/eval_jaxpr/ppermute | solution.py:18
  241.8 23.5 %collective-permute-start = (f32[2,3,8,1,1024]{4,3,2,1,0:T(1,128)}, f32[2,3,8,1,1024]{4,3,2,1,0:T(1,128)}, u32[]{:S(2)}, u32[]{:S(2)}) collective-permute-start(f32[2,3,8,1,1024]{4,3,2,1,0:T(1,128)} %get-tuple-element.1433), channel_id=1, source_target_pairs={{0,1},{1,2},{2,3},{3,0},{4,5},{5,6},{6,7},{7,4},{8,9},{9,10},{10,1... | collective-permute-start | bytes 589832 | tf_op jit(solution)/shard_map/while/body/eval_jaxpr/ppermute | solution.py:15
  277.8 7.7 %collective-permute-start.3 = (f32[2,3,8,1,1024]{4,3,2,1,0:T(1,128)S(1)}, f32[2,3,8,1,1024]{4,3,2,1,0:T(1,128)S(1)}, u32[]{:S(2)}, u32[]{:S(2)}) collective-permute-start(f32[2,3,8,1,1024]{4,3,2,1,0:T(1,128)S(1)} %get-tuple-element.1562), channel_id=1, source_target_pairs={{1,0},{2,1},{3,2},{0,3},{5,4},{6,5},{7,6},{4,7},{9,8},{10,9},{11,1... | collective-permute-start | bytes 589832 | tf_op jit(solution)/shard_map/while/body/eval_jaxpr/ppermute | solution.py:18
  281.4 7.9 %collective-permute-start.2 = (f32[2,3,8,1,1024]{4,3,2,1,0:T(1,128)S(1)}, f32[2,3,8,1,1024]{4,3,2,1,0:T(1,128)S(1)}, u32[]{:S(2)}, u32[]{:S(2)}) collective-permute-start(f32[2,3,8,1,1024]{4,3,2,1,0:T(1,128)S(1)} %get-tuple-element.1549), channel_id=1, source_target_pairs={{0,1},{1,2},{2,3},{3,0},{4,5},{5,6},{6,7},{7,4},{8,9},{9,10},{10,1... | collective-permute-start | bytes 589832 | tf_op jit(solution)/shard_map/while/body/eval_jaxpr/ppermute | solution.py:15
  290.3 9.4 %copy-start.3 = (f32[2,3,8,2,1024]{4,3,2,1,0:T(2,128)S(1)}, f32[2,3,8,2,1024]{4,3,2,1,0:T(2,128)}, u32[]{:S(2)}) copy-start(f32[2,3,8,2,1024]{4,3,2,1,0:T(2,128)} %copy-done.2) | copy-start | bytes 1179652 | tf_op jit(solution)/shard_map/while
  291.6 8.2 %collective-permute-start.4 = (f32[2,3,8,2,1024]{4,3,2,1,0:T(2,128)S(1)}, f32[2,3,8,2,1024]{4,3,2,1,0:T(2,128)S(1)}, u32[]{:S(2)}, u32[]{:S(2)}) collective-permute-start(f32[2,3,8,2,1024]{4,3,2,1,0:T(2,128)S(1)} %get-tuple-element.1575), channel_id=1, source_target_pairs={{0,4},{4,8},{8,12},{12,16},{16,20},{20,24},{24,28},{28,0},{1,5},{5... | collective-permute-start | bytes 1179656 | tf_op jit(solution)/shard_map/while/body/eval_jaxpr/ppermute | solution.py:25
  301.9 22.8 %collective-permute-start.1 = (f32[2,3,8,1,1024]{4,3,2,1,0:T(1,128)}, f32[2,3,8,1,1024]{4,3,2,1,0:T(1,128)}, u32[]{:S(2)}, u32[]{:S(2)}) collective-permute-start(f32[2,3,8,1,1024]{4,3,2,1,0:T(1,128)} %get-tuple-element.1466), channel_id=1, source_target_pairs={{1,0},{2,1},{3,2},{0,3},{5,4},{6,5},{7,6},{4,7},{9,8},{10,9},{11,1... | collective-permute-start | bytes 589832 | tf_op jit(solution)/shard_map/while/body/eval_jaxpr/ppermute | solution.py:18
  303.8 23.4 %collective-permute-start = (f32[2,3,8,1,1024]{4,3,2,1,0:T(1,128)}, f32[2,3,8,1,1024]{4,3,2,1,0:T(1,128)}, u32[]{:S(2)}, u32[]{:S(2)}) collective-permute-start(f32[2,3,8,1,1024]{4,3,2,1,0:T(1,128)} %get-tuple-element.1433), channel_id=1, source_target_pairs={{0,1},{1,2},{2,3},{3,0},{4,5},{5,6},{6,7},{7,4},{8,9},{9,10},{10,1... | collective-permute-start | bytes 589832 | tf_op jit(solution)/shard_map/while/body/eval_jaxpr/ppermute | solution.py:15
  339.6 7.5 %collective-permute-start.3 = (f32[2,3,8,1,1024]{4,3,2,1,0:T(1,128)S(1)}, f32[2,3,8,1,1024]{4,3,2,1,0:T(1,128)S(1)}, u32[]{:S(2)}, u32[]{:S(2)}) collective-permute-start(f32[2,3,8,1,1024]{4,3,2,1,0:T(1,128)S(1)} %get-tuple-element.1562), channel_id=1, source_target_pairs={{1,0},{2,1},{3,2},{0,3},{5,4},{6,5},{7,6},{4,7},{9,8},{10,9},{11,1... | collective-permute-start | bytes 589832 | tf_op jit(solution)/shard_map/while/body/eval_jaxpr/ppermute | solution.py:18
  343.3 7.5 %collective-permute-start.2 = (f32[2,3,8,1,1024]{4,3,2,1,0:T(1,128)S(1)}, f32[2,3,8,1,1024]{4,3,2,1,0:T(1,128)S(1)}, u32[]{:S(2)}, u32[]{:S(2)}) collective-permute-start(f32[2,3,8,1,1024]{4,3,2,1,0:T(1,128)S(1)} %get-tuple-element.1549), channel_id=1, source_target_pairs={{0,1},{1,2},{2,3},{3,0},{4,5},{5,6},{6,7},{7,4},{8,9},{9,10},{10,1... | collective-permute-start | bytes 589832 | tf_op jit(solution)/shard_map/while/body/eval_jaxpr/ppermute | solution.py:15
  353.2 8.2 %collective-permute-start.4 = (f32[2,3,8,2,1024]{4,3,2,1,0:T(2,128)S(1)}, f32[2,3,8,2,1024]{4,3,2,1,0:T(2,128)S(1)}, u32[]{:S(2)}, u32[]{:S(2)}) collective-permute-start(f32[2,3,8,2,1024]{4,3,2,1,0:T(2,128)S(1)} %get-tuple-element.1575), channel_id=1, source_target_pairs={{0,4},{4,8},{8,12},{12,16},{16,20},{20,24},{24,28},{28,0},{1,5},{5... | collective-permute-start | bytes 1179656 | tf_op jit(solution)/shard_map/while/body/eval_jaxpr/ppermute | solution.py:25
  363.5 22.8 %collective-permute-start.1 = (f32[2,3,8,1,1024]{4,3,2,1,0:T(1,128)}, f32[2,3,8,1,1024]{4,3,2,1,0:T(1,128)}, u32[]{:S(2)}, u32[]{:S(2)}) collective-permute-start(f32[2,3,8,1,1024]{4,3,2,1,0:T(1,128)} %get-tuple-element.1466), channel_id=1, source_target_pairs={{1,0},{2,1},{3,2},{0,3},{5,4},{6,5},{7,6},{4,7},{9,8},{10,9},{11,1... | collective-permute-start | bytes 589832 | tf_op jit(solution)/shard_map/while/body/eval_jaxpr/ppermute | solution.py:18
  364.8 23.9 %collective-permute-start = (f32[2,3,8,1,1024]{4,3,2,1,0:T(1,128)}, f32[2,3,8,1,1024]{4,3,2,1,0:T(1,128)}, u32[]{:S(2)}, u32[]{:S(2)}) collective-permute-start(f32[2,3,8,1,1024]{4,3,2,1,0:T(1,128)} %get-tuple-element.1433), channel_id=1, source_target_pairs={{0,1},{1,2},{2,3},{3,0},{4,5},{5,6},{6,7},{7,4},{8,9},{9,10},{10,1... | collective-permute-start | bytes 589832 | tf_op jit(solution)/shard_map/while/body/eval_jaxpr/ppermute | solution.py:15
  401.2 7.1 %collective-permute-start.3 = (f32[2,3,8,1,1024]{4,3,2,1,0:T(1,128)S(1)}, f32[2,3,8,1,1024]{4,3,2,1,0:T(1,128)S(1)}, u32[]{:S(2)}, u32[]{:S(2)}) collective-permute-start(f32[2,3,8,1,1024]{4,3,2,1,0:T(1,128)S(1)} %get-tuple-element.1562), channel_id=1, source_target_pairs={{1,0},{2,1},{3,2},{0,3},{5,4},{6,5},{7,6},{4,7},{9,8},{10,9},{11,1... | collective-permute-start | bytes 589832 | tf_op jit(solution)/shard_map/while/body/eval_jaxpr/ppermute | solution.py:18
  404.4 7.9 %collective-permute-start.2 = (f32[2,3,8,1,1024]{4,3,2,1,0:T(1,128)S(1)}, f32[2,3,8,1,1024]{4,3,2,1,0:T(1,128)S(1)}, u32[]{:S(2)}, u32[]{:S(2)}) collective-permute-start(f32[2,3,8,1,1024]{4,3,2,1,0:T(1,128)S(1)} %get-tuple-element.1549), channel_id=1, source_target_pairs={{0,1},{1,2},{2,3},{3,0},{4,5},{5,6},{6,7},{7,4},{8,9},{9,10},{10,1... | collective-permute-start | bytes 589832 | tf_op jit(solution)/shard_map/while/body/eval_jaxpr/ppermute | solution.py:15
  414.7 8.2 %collective-permute-start.4 = (f32[2,3,8,2,1024]{4,3,2,1,0:T(2,128)S(1)}, f32[2,3,8,2,1024]{4,3,2,1,0:T(2,128)S(1)}, u32[]{:S(2)}, u32[]{:S(2)}) collective-permute-start(f32[2,3,8,2,1024]{4,3,2,1,0:T(2,128)S(1)} %get-tuple-element.1575), channel_id=1, source_target_pairs={{0,4},{4,8},{8,12},{12,16},{16,20},{20,24},{24,28},{28,0},{1,5},{5... | collective-permute-start | bytes 1179656 | tf_op jit(solution)/shard_map/while/body/eval_jaxpr/ppermute | solution.py:25
  425.0 22.8 %collective-permute-start.1 = (f32[2,3,8,1,1024]{4,3,2,1,0:T(1,128)}, f32[2,3,8,1,1024]{4,3,2,1,0:T(1,128)}, u32[]{:S(2)}, u32[]{:S(2)}) collective-permute-start(f32[2,3,8,1,1024]{4,3,2,1,0:T(1,128)} %get-tuple-element.1466), channel_id=1, source_target_pairs={{1,0},{2,1},{3,2},{0,3},{5,4},{6,5},{7,6},{4,7},{9,8},{10,9},{11,1... | collective-permute-start | bytes 589832 | tf_op jit(solution)/shard_map/while/body/eval_jaxpr/ppermute | solution.py:18
  426.5 23.6 %collective-permute-start = (f32[2,3,8,1,1024]{4,3,2,1,0:T(1,128)}, f32[2,3,8,1,1024]{4,3,2,1,0:T(1,128)}, u32[]{:S(2)}, u32[]{:S(2)}) collective-permute-start(f32[2,3,8,1,1024]{4,3,2,1,0:T(1,128)} %get-tuple-element.1433), channel_id=1, source_target_pairs={{0,1},{1,2},{2,3},{3,0},{4,5},{5,6},{6,7},{7,4},{8,9},{9,10},{10,1... | collective-permute-start | bytes 589832 | tf_op jit(solution)/shard_map/while/body/eval_jaxpr/ppermute | solution.py:15
  462.7 7.4 %collective-permute-start.3 = (f32[2,3,8,1,1024]{4,3,2,1,0:T(1,128)S(1)}, f32[2,3,8,1,1024]{4,3,2,1,0:T(1,128)S(1)}, u32[]{:S(2)}, u32[]{:S(2)}) collective-permute-start(f32[2,3,8,1,1024]{4,3,2,1,0:T(1,128)S(1)} %get-tuple-element.1562), channel_id=1, source_target_pairs={{1,0},{2,1},{3,2},{0,3},{5,4},{6,5},{7,6},{4,7},{9,8},{10,9},{11,1... | collective-permute-start | bytes 589832 | tf_op jit(solution)/shard_map/while/body/eval_jaxpr/ppermute | solution.py:18
  466.1 7.9 %collective-permute-start.2 = (f32[2,3,8,1,1024]{4,3,2,1,0:T(1,128)S(1)}, f32[2,3,8,1,1024]{4,3,2,1,0:T(1,128)S(1)}, u32[]{:S(2)}, u32[]{:S(2)}) collective-permute-start(f32[2,3,8,1,1024]{4,3,2,1,0:T(1,128)S(1)} %get-tuple-element.1549), channel_id=1, source_target_pairs={{0,1},{1,2},{2,3},{3,0},{4,5},{5,6},{6,7},{7,4},{8,9},{9,10},{10,1... | collective-permute-start | bytes 589832 | tf_op jit(solution)/shard_map/while/body/eval_jaxpr/ppermute | solution.py:15
  475.1 9.4 %copy-start.3 = (f32[2,3,8,2,1024]{4,3,2,1,0:T(2,128)S(1)}, f32[2,3,8,2,1024]{4,3,2,1,0:T(2,128)}, u32[]{:S(2)}) copy-start(f32[2,3,8,2,1024]{4,3,2,1,0:T(2,128)} %copy-done.2) | copy-start | bytes 1179652 | tf_op jit(solution)/shard_map/while
  476.4 8.2 %collective-permute-start.4 = (f32[2,3,8,2,1024]{4,3,2,1,0:T(2,128)S(1)}, f32[2,3,8,2,1024]{4,3,2,1,0:T(2,128)S(1)}, u32[]{:S(2)}, u32[]{:S(2)}) collective-permute-start(f32[2,3,8,2,1024]{4,3,2,1,0:T(2,128)S(1)} %get-tuple-element.1575), channel_id=1, source_target_pairs={{0,4},{4,8},{8,12},{12,16},{16,20},{20,24},{24,28},{28,0},{1,5},{5... | collective-permute-start | bytes 1179656 | tf_op jit(solution)/shard_map/while/body/eval_jaxpr/ppermute | solution.py:25
  495.7 8.2 %collective-permute-start.7 = (f32[2,3,8,1,1024]{4,2,3,1,0:T(8,128)S(1)}, f32[2,3,8,1,1024]{4,2,3,1,0:T(8,128)S(1)}, u32[]{:S(2)}, u32[]{:S(2)}) collective-permute-start(f32[2,3,8,1,1024]{4,2,3,1,0:T(8,128)S(1)} %get-tuple-element.784), channel_id=1, source_target_pairs={{0,1},{1,2},{2,3},{3,0},{4,5},{5,6},{6,7},{7,4},{8,9},{9,10},{10,1... | collective-permute-start | bytes 589832 | tf_op jit(solution)/shard_map/ppermute | solution.py:15
  496.5 9.2 %collective-permute-start.6 = (f32[2,3,8,1,1024]{4,2,3,1,0:T(8,128)S(1)}, f32[2,3,8,1,1024]{4,2,3,1,0:T(8,128)S(1)}, u32[]{:S(2)}, u32[]{:S(2)}) collective-permute-start(f32[2,3,8,1,1024]{4,2,3,1,0:T(8,128)S(1)} %get-tuple-element.785), channel_id=1, source_target_pairs={{1,0},{2,1},{3,2},{0,3},{5,4},{6,5},{7,6},{4,7},{9,8},{10,9},{11,1... | collective-permute-start | bytes 589832 | tf_op jit(solution)/shard_map/ppermute | solution.py:18
  509.7 9.6 %collective-permute-start.9 = (f32[2,3,8,1,1024]{4,2,3,1,0:T(8,128)S(1)}, f32[2,3,8,1,1024]{4,2,3,1,0:T(8,128)S(1)}, u32[]{:S(2)}, u32[]{:S(2)}) collective-permute-start(f32[2,3,8,1,1024]{4,2,3,1,0:T(8,128)S(1)} %get-tuple-element.766), channel_id=1, source_target_pairs={{0,1},{1,2},{2,3},{3,0},{4,5},{5,6},{6,7},{7,4},{8,9},{9,10},{10,1... | collective-permute-start | bytes 589832 | tf_op jit(solution)/shard_map/ppermute | solution.py:15
  510.1 10.3 %collective-permute-start.8 = (f32[2,3,8,1,1024]{4,2,3,1,0:T(8,128)S(1)}, f32[2,3,8,1,1024]{4,2,3,1,0:T(8,128)S(1)}, u32[]{:S(2)}, u32[]{:S(2)}) collective-permute-start(f32[2,3,8,1,1024]{4,2,3,1,0:T(8,128)S(1)} %get-tuple-element.767), channel_id=1, source_target_pairs={{1,0},{2,1},{3,2},{0,3},{5,4},{6,5},{7,6},{4,7},{9,8},{10,9},{11,1... | collective-permute-start | bytes 589832 | tf_op jit(solution)/shard_map/ppermute | solution.py:18
  (985 other events, 2014.7 us)
Sparse Core Ops, SparseCore 0:
  528.6 17.2 reduce-scatter.3
where the time goes:
time: 561 us; the launch traced here: 555 us
  other arithmetic  188 us (34%)
  waiting for transfers between devices  126 us (22%)
  local copies, waits for them, and re-layouts  125 us (22%)
  starting transfers between devices  51.2 us (9%)
  loops' own time  48 us (9%)
  between operations  14.5 us (3%)
    ppermute x8, waiting for transfers between devices, shifted(): lax.ppermute(x, axis, [(i, (i + by) % length) for i in range(length)])  56.6 us
    add x144, other arithmetic, colour_adjoint(): real_sum + matrix[0, in_colour, out_colour] * vector_in[0, in_colour]  55.7 us
    another operation x1, loops' own time, local(): state_pair = lax.fori_loop(0, n_time - 1, loop_round, (empty, empty))  48 us
    ppermute x16, starting transfers between devices, padded(): lax.ppermute(lax.slice_in_dim(block, 0, width, axis=dim), axis, backward)  44.8 us
    sub x144, other arithmetic, colour_apply(): real_sum + matrix[0, out_colour, in_colour] * vector_in[0, in_colour]  39.8 us
    another operation x154, other arithmetic, colour_adjoint(): return jnp.stack([jnp.stack(real_rows), jnp.stack(imag_rows)])  27.1 us
    ppermute x16, waiting for transfers between devices, padded(): lax.ppermute(lax.slice_in_dim(block, 0, width, axis=dim), axis, backward)  26.2 us
    ppermute x16, waiting for transfers between devices, padded(): lax.ppermute(lax.slice_in_dim(block, block.shape[dim] - width, None, axis...  25.5 us
  transfers between devices with their start and end apart: 41, of which 26 were waited for; matrix products, arithmetic and copies ran while one was open for 32% of the time, Pallas kernels for 0%

commit v1 on v0

v1 whole, which is shorter than its diff:
```python
import math

import jax
import jax.numpy as jnp
from jax import lax
from jax.experimental import pallas as pl
from jax.experimental.pallas import tpu as pltpu
from jax.sharding import PartitionSpec as P

LANES = 128


def roll(x, by, axis):
    size = x.shape[axis]
    return pltpu.roll(x, by % size, axis)


def apply_link(link, vec):
    real, imag = [], []
    for a in range(3):
        re = im = None
        for b in range(3):
            ur, ui = link(0, a, b), link(1, a, b)
            r = ur * vec[0][b] - ui * vec[1][b]
            i = ur * vec[1][b] + ui * vec[0][b]
            re = r if re is None else re + r
            im = i if im is None else im + i
        real.append(re)
        imag.append(im)
    return [real, imag]


def apply_both(link, vec_up, vec_here):
    up = [[None] * 3, [None] * 3]
    down = [[None] * 3, [None] * 3]

    def add(out, part, at, value):
        out[part][at] = value if out[part][at] is None else out[part][at] + value

    for a in range(3):
        for b in range(3):
            ur, ui = link(0, a, b), link(1, a, b)
            add(up, 0, a, ur * vec_up[0][b] - ui * vec_up[1][b])
            add(up, 1, a, ur * vec_up[1][b] + ui * vec_up[0][b])
            add(down, 0, b, ur * vec_here[0][a] + ui * vec_here[1][a])
            add(down, 1, b, ur * vec_here[1][a] - ui * vec_here[0][a])
    return up, down


def evolve_kernel(planes, rows, blocks, side, start_ref, place_ref, weight_ref, gauge_ref, time_ref,
                  source_ref, out_ref, field, turned):
    which, rounds = pl.program_id(0), pl.program_id(1)
    extent = planes * blocks
    weight = weight_ref[which]
    lane = lax.broadcasted_iota(jnp.int32, (planes, rows, LANES), 2)
    per_row = LANES // side

    def y_up(x):
        turned_lanes = roll(x, -side, 2)
        return jnp.where(lane < LANES - side, turned_lanes, roll(turned_lanes, -1, 1))

    def y_down(x):
        turned_lanes = roll(x, side, 2)
        return jnp.where(lane >= side, turned_lanes, roll(turned_lanes, 1, 1))

    def z_up(x):
        return jnp.where(lane % side == side - 1, roll(x, side - 1, 2), roll(x, -1, 2))

    def z_down(x):
        return jnp.where(lane % side == 0, roll(x, 1 - side, 2), roll(x, 1, 2))

    def gauge(block, direction):
        def link(part, row, column):
            at = ((part * 3 + direction) * 3 + row) * 3 + column
            value = gauge_ref[0, block, at].astype(jnp.float32)
            return value.reshape(planes, rows, LANES)
        return link

    def read(ref, first):
        return [[ref[part * 3 + c, pl.ds(first, planes)] for c in range(3)] for part in range(2)]

    def each(fn, vec):
        return [[fn(vec[part][c]) for c in range(3)] for part in range(2)]

    def plus(*vecs):
        return [[sum(v[part][c] for v in vecs[1:]) + vecs[0][part][c] for c in range(3)] for part in range(2)]

    def close(ref):
        for at in range(6):
            ref[at, pl.ds(extent, 1)] = ref[at, pl.ds(0, 1)]

    def hop(src, dst, then):
        last = read(src, extent - planes)
        _, wrapped = apply_both(gauge(blocks - 1, 0), last, last)
        carried = tuple(wrapped[part][c][planes - 1:] for part in range(2) for c in range(3))

        def one_block(block, carry):
            first = block * planes
            here = read(src, first)
            up, down = apply_both(gauge(block, 0), read(src, first + 1), here)
            flat = [down[part][c] for part in range(2) for c in range(3)]
            moved = [jnp.concatenate([low, x[: planes - 1]], axis=0) for low, x in zip(carry, flat)]
            total = plus(up, [moved[:3], moved[3:]])
            up, down = apply_both(gauge(block, 1), each(y_up, here), here)
            total = plus(total, up, each(y_down, down))
            up, down = apply_both(gauge(block, 2), each(z_up, here), here)
            total = plus(total, up, each(z_down, down))
            result = [[here[part][c] + weight * (total[part][c] - 6.0 * here[part][c]) for c in range(3)]
                      for part in range(2)]
            result = then(block, result)
            for part in range(2):
                for c in range(3):
                    dst[part * 3 + c, pl.ds(first, planes)] = result[part][c]
            return tuple(x[planes - 1:] for x in flat)

        lax.fori_loop(0, blocks, one_block, carried)
        close(dst)

    def through_time(block, vec):
        u = [[[time_ref[0, block, (part * 2 + row) * 3 + c].reshape(planes, rows, LANES) for c in range(3)]
              for row in range(2)] for part in range(2)]
        third = [[], []]
        for c in range(3):
            d, e = (c + 1) % 3, (c + 2) % 3
            third[0].append(u[0][0][d] * u[0][1][e] - u[1][0][d] * u[1][1][e]
                            - u[0][0][e] * u[0][1][d] + u[1][0][e] * u[1][1][d])
            third[1].append(-(u[0][0][d] * u[1][1][e] + u[1][0][d] * u[0][1][e]
                              - u[0][0][e] * u[1][1][d] - u[1][0][e] * u[0][1][d]))
        u[0].append(third[0])
        u[1].append(third[1])
        real, imag = [], []
        for c in range(3):
            real.append(sum(u[0][row][c] * vec[0][row] + u[1][row][c] * vec[1][row] for row in range(3)))
            imag.append(sum(u[0][row][c] * vec[1][row] - u[1][row][c] * vec[0][row] for row in range(3)))
        return [real, imag]

    @pl.when(rounds == 0)
    def _():
        for block in range(blocks):
            for at in range(6):
                value = source_ref[0, block, at].astype(jnp.float32)
                field[at, pl.ds(block * planes, planes)] = value.reshape(planes, rows, LANES)
        close(field)

    hop(field, turned, through_time)
    hop(turned, field, lambda block, vec: vec)
    mine = place_ref[0] * planes
    for at in range(6):
        value = field[at, pl.ds(mine, planes)].reshape(planes * rows, LANES)
        out_ref[0, 0, at] = value.astype(jnp.bfloat16)


def evolve(gauge_all, time_all, sources, starts, place, weights, n_time):
    held, blocks = sources.shape[0], sources.shape[1]
    tile = sources.shape[3]
    planes = evolve.planes
    rows = tile // planes
    side = math.isqrt(rows * LANES)

    def at_time(v, r, start, place):
        return (lax.rem(start[v] + r, n_time), 0, 0, 0, 0)

    kernel = lambda *refs: evolve_kernel(planes, rows, blocks, side, *refs)
    extent = planes * blocks
    return pl.pallas_call(
        kernel,
        out_shape=jax.ShapeDtypeStruct((held, n_time, 6, tile, LANES), jnp.bfloat16),
        grid_spec=pltpu.PrefetchScalarGridSpec(
            num_scalar_prefetch=2,
            grid=(held, n_time),
            in_specs=[
                pl.BlockSpec(memory_space=pltpu.SMEM),
                pl.BlockSpec((1,) + gauge_all.shape[1:], at_time),
                pl.BlockSpec((1,) + time_all.shape[1:], at_time),
                pl.BlockSpec((1,) + sources.shape[1:], lambda v, r, start, place: (v, 0, 0, 0, 0)),
            ],
            out_specs=pl.BlockSpec(
                (1, 1, 6, tile, LANES),
                lambda v, r, start, place: (v, lax.rem(start[v] + r, n_time), 0, 0, 0)),
            scratch_shapes=[pltpu.VMEM((6, extent + 1, rows, LANES), jnp.float32)] * 2,
        ),
        name="evolve",
    )(starts, place, weights, gauge_all, time_all, sources)


def project(sinks, rounded):
    def dot(a, b):
        return jnp.einsum("ecxs,vcxs->ve", a, b, preferred_element_type=jnp.float32)

    real_part = dot(sinks[0], rounded[:, 0]) + dot(sinks[1], rounded[:, 1])
    imag_part = dot(sinks[0], rounded[:, 1]) - dot(sinks[1], rounded[:, 0])
    return jnp.stack([real_part, imag_part])


def local(gauge_links, time_links, sink_vectors, source_times, source_index, kinetic_coef):
    planes, sites = gauge_links.shape[5:]
    tile = planes * sites // LANES
    n_time = lax.axis_size("tm")
    blocks = lax.axis_size("space")
    my_time = lax.axis_index("tm")
    groups, per_group = kinetic_coef.shape
    count = groups * per_group
    held = -(-count // n_time)
    fill = (0, held * n_time - count)
    start_flat = jnp.pad(jnp.repeat(source_times, per_group), fill)
    index_flat = jnp.pad(source_index.reshape(-1), fill)
    coef_flat = jnp.pad(kinetic_coef.reshape(-1), fill)
    my_sinks = sink_vectors[0]

    def gather(x):
        whole = lax.all_gather(x, ("tm", "space"), axis=0, tiled=False)
        return whole.reshape((n_time, blocks) + x.shape)

    gauge_all = gather(gauge_links.astype(jnp.bfloat16).reshape(54, tile, LANES))
    time_all = gather(time_links[0, :, :2].reshape(12, tile, LANES))

    mine = lambda x: lax.dynamic_slice_in_dim(x, my_time * held, held)
    starts = mine(start_flat)
    picked = jnp.take(my_sinks, index_flat, axis=1)
    picked = jnp.moveaxis(picked, 1, 0).reshape(n_time, held, 6, tile, LANES)
    sent = lax.all_to_all(picked, "tm", 0, 0, tiled=False)
    chosen = jnp.stack([lax.dynamic_index_in_dim(sent[:, v], starts[v], 0, keepdims=False)
                        for v in range(held)])
    sources = jnp.moveaxis(lax.all_gather(chosen, "space", axis=0, tiled=False), 0, 1)

    evolve.planes = planes
    place = lax.axis_index("space").astype(jnp.int32)[None]
    evolved = evolve(gauge_all, time_all, sources, starts, place, 0.5 * mine(coef_flat), n_time)
    back = lax.all_to_all(jnp.moveaxis(evolved, 1, 0), "tm", 0, 0, tiled=False)
    rounded = back.reshape(n_time * held, 2, 3, planes, sites)[:count]
    correlations = project(my_sinks, rounded)
    correlations = correlations.reshape(2, groups, per_group, 1, my_sinks.shape[1])
    return lax.psum_scatter(correlations, "space", scatter_dimension=4, tiled=True)


def solution(mesh):
    placed = (
        P("tm", None, None, None, None, "space", None),
        P("tm", None, None, None, "space", None),
        P("tm", None, None, None, "space", None),
        P(),
        P(),
        P(),
    )
    return jax.shard_map(
        local,
        mesh=mesh,
        in_specs=placed,
        out_specs=P(None, None, None, "tm", "space"),
        check_vma=False,
    )
```

time: 561 us -> 202 us (0.36); the launches traced: 555 us -> 202 us
  other arithmetic: 188 us -> 1.45 us
  local copies, waits for them, and re-layouts: 125 us -> 17.3 us
  loops' own time: 48 us -> 0 us
  starting transfers between devices: 51.2 us -> 8.67 us
  Pallas kernels: 0 us -> 14.3 us
  blocking collectives: 0 us -> 14.3 us
    ppermute x40 -> x0, waiting for transfers between devices: 108 us -> none  [the longest x8 56.6 us: shifted(): lax.ppermute(x, axis, [(i, (i + by) % length) for i in range(length)])]
    all_gather x0 -> x2, waiting for transfers between devices: none -> 105 us  [gather(): whole = lax.all_gather(x, ('tm', 'space'), axis=0, tiled=False)]
    add x152 -> x0, other arithmetic: 62.9 us -> none  [the longest x144 55.7 us: colour_adjoint(): real_sum + matrix[0, in_colour, out_colour] * vector_in[0, in_colour]]
    ppermute x40 -> x0, starting transfers between devices: 51.2 us -> none  [the longest x16 44.8 us: padded(): lax.ppermute(lax.slice_in_dim(block, 0, width, axis=dim), axis, backward)]
    another operation x1 -> x0, loops' own time: 48 us -> none  [local(): state_pair = lax.fori_loop(0, n_time - 1, loop_round, (empty, empty))]
    sub x169 -> x0, other arithmetic: 44.7 us -> none  [the longest x144 39.8 us: colour_apply(): real_sum + matrix[0, out_colour, in_colour] * vector_in[0, in_colour]]
    mul x58 -> x0, local copies, waits for them, and re-layouts: 36.8 us -> none  [the longest x24 15.4 us: colour_adjoint(): matrix[0, 0, out_colour] * vector_in[0, 0]]
    slice x64 -> x3, local copies, waits for them, and re-layouts: 41.4 us -> 4.93 us  [the longest x2 4.02 us: project(): real_part = dot(sinks[0], rounded[:, 0]) + dot(sinks[1], rounded[:, 1])]
  transfers between devices with their start and end apart: 41 -> 5, of which waited for: 26 -> 5; matrix products, arithmetic and copies ran while one was open for 32% -> 6% of each run, Pallas kernels for 0% -> 0%
where the time goes in v1:
time: 202 us
  waiting for transfers between devices  128 us (63%)
  local copies, waits for them, and re-layouts  17.3 us (9%)
  between operations  15.8 us (8%)
  blocking collectives  14.3 us (7%)
  Pallas kernels  14.3 us (7%)
  starting transfers between devices  8.67 us (4%)
  matrix products  2.2 us (1%)
    all_gather x2, waiting for transfers between devices, gather(): whole = lax.all_gather(x, ('tm', 'space'), axis=0, tiled=False)  105 us
    unnamed x4, waiting for transfers between devices  17.2 us
    pallas_call x1, Pallas kernels, evolve(): pl.pallas_call(kernel, out_shape=jax.ShapeDtypeStruct((held, n_time, 6, t...  14.3 us
    all_gather x1, blocking collectives, local(): lax.all_gather(chosen, 'space', axis=0, tiled=False)  14.3 us
    unnamed x13, local copies, waits for them, and re-layouts  5.49 us
    all_to_all x1, starting transfers between devices, local(): sent = lax.all_to_all(picked, 'tm', 0, 0, tiled=False)  5.2 us
  transfers between devices with their start and end apart: 5, of which 5 were waited for; matrix products, arithmetic and copies ran while one was open for 6% of the time, Pallas kernels for 0%

profile of v1, /device:TPU:0, one launch (start us, length us, event | category | flops | bytes accessed | tf_op | source)
XLA Modules:
  0.0 201.6 jit_solution(5552414973807834)
XLA Ops:
  6.5 0.0 all-gather.5.cloned.1.call-start
  6.5 0.9 slice.21
  7.5 0.0 copy-start.2
  7.5 0.7 all_gather_reshape_squeeze.3
  8.2 0.0 copy-start.1
  8.2 0.0 all-gather.5.cloned.1.call-update
  8.2 0.0 all-gather.3.cloned.1.call-start
  8.3 1.2 convert_element_type.3
  9.4 0.8 all_gather_reshape.3
  10.3 0.0 all-gather.3.cloned.1.call-update
  10.3 0.0 copy-done
  10.3 0.1 copy.34
  10.4 0.1 reshape.74
  10.5 0.1 reshape.73
  10.6 2.8 %gather_fusion = bf16[8,2,3,2,1024]{4,3,2,1,0:T(2,128)(2,1)S(1)} fusion(bf16[2,128,3,2,1024]{4,3,2,1,0:T(2,128)(2,1)} %bitcast.71, s32[1024]{0:T(1024)S(1)} %pad_clamp_fusion), kind=kCustom, calls=%fused_computation | custom fusion | bytes 393248 | tf_op jit(solution)/shard_map/jit(_take)/gather | solution.py:219
  13.4 0.2 broadcast_select_fusion
  13.7 0.8 reshape.75
  14.5 5.2 %all-to-all-start = ((bf16[8,1,6,16,128]{4,3,2,1,0:T(8,128)(2,1)}), bf16[8,1,6,16,128]{4,3,2,1,0:T(8,128)(2,1)S(1)}, u32[]{:S(2)}, u32[]{:S(2)}) async-start(bf16[8,1,6,16,128]{4,3,2,1,0:T(8,128)(2,1)} %reshape.75), calls=%async_computation | async-start | bytes 393216 | tf_op jit(solution)/shard_map/all_to_all | solution.py:221
  19.7 0.0 copy-done.2
  19.7 0.1 broadcast_in_dim.16
  19.8 0.1 reshape.69
  19.8 0.6 dynamic_slice.10.refs_0_
  21.7 0.0 copy-done.1
  21.7 0.1 copy.33
  21.8 0.1 reshape.70
  21.9 0.6 dynamic_slice.11
  23.8 2.8 %all-to-all-done = bf16[8,1,6,16,128]{4,3,2,1,0:T(8,128)(2,1)S(1)} async-done(((bf16[8,1,6,16,128]{4,3,2,1,0:T(8,128)(2,1)}), bf16[8,1,6,16,128]{4,3,2,1,0:T(8,128)(2,1)S(1)}, u32[]{:S(2)}, u32[]{:S(2)}) %all-to-all-start) | async-done | bytes 196640 | tf_op jit(solution)/shard_map/all_to_all | solution.py:221
  26.6 14.3 %all_gather.11 = bf16[4,1,6,16,128]{4,3,2,1,0:T(8,128)(2,1)} all-gather(bf16[1,1,6,16,128]{4,3,2,1,0:T(8,128)(2,1)S(1)} %constant_dynamic-slice_fusion), channel_id=1, replica_groups=mesh['tm'=8,'space'=4] {'space'}, dimensions={0}, use_global_device_ids=true | all-gather | bytes 122880 | tf_op jit(solution)/shard_map/all_gather | solution.py:224
  40.8 31.8 %all-gather.5.cloned.1.call-done = f32[32,12,16,128]{3,2,1,0:T(8,128)} async-done(((f32[1,12,16,128]{3,2,1,0:T(8,128)}), f32[32,12,16,128]{3,2,1,0:T(8,128)}) %all-gather.5.cloned.1.call-update) | async-done | bytes 3145744 | tf_op jit(solution)/shard_map/all_gather | solution.py:211
  72.6 73.7 %all-gather.3.cloned.1.call-done = bf16[32,54,16,128]{3,2,1,0:T(8,128)(2,1)} async-done(((bf16[1,54,16,128]{3,2,1,0:T(8,128)(2,1)}), bf16[32,54,16,128]{3,2,1,0:T(8,128)(2,1)}) %all-gather.3.cloned.1.call-update) | async-done | bytes 7077904 | tf_op jit(solution)/shard_map/all_gather | solution.py:211
  146.3 14.3 %evolve.1 = bf16[1,8,6,16,128]{4,3,2,1,0:T(8,128)(2,1)} custom-call(s32[1]{0:T(128)} %dynamic_slice.10.refs_0_, s32[1]{0:T(128)} %bitcast.refs_1_, f32[1]{0:T(128)S(6)} %mul.3.refs_2_, bf16[8,4,54,16,128]{4,3,2,1,0:T(8,128)(2,1)} %bitcast.70, f32[8,4,12,16,128]{4,3,2,1,0:T(8,128)} %bitcast.72, bf16[1,4,6,16,128]{4,3,2,1,0:T(8,128)(2,1)} %bitcast.75), custom_call_target="tpu_custom_call" | custom-call | tf_op jit(solution)/shard_map/evolve/pallas_call | solution.py:165
  160.6 3.4 %all-to-all-start.1 = ((bf16[8,1,6,16,128]{4,3,2,1,0:T(8,128)(2,1)}), bf16[8,1,6,16,128]{4,3,2,1,0:T(8,128)(2,1)S(1)}, u32[]{:S(2)}, u32[]{:S(2)}) async-start(bf16[8,1,6,16,128]{4,3,2,1,0:T(8,128)(2,1)} %bitcast.74), calls=%async_computation.1 | async-start | bytes 393216 | tf_op jit(solution)/shard_map/all_to_all | solution.py:229
  164.0 0.0 reduce-scatter.4.cloned.1.call-start
  164.1 3.9 %fusion.11 = (bf16[1,1,128,3,2,1024]{5,4,3,2,1,0:T(2,128)(2,1)S(1)}, bf16[1,1,128,3,2,1024]{5,4,3,2,1,0:T(2,128)(2,1)S(1)}) fusion(bf16[1,2,128,3,2,1024]{5,4,3,2,1,0:T(2,128)(2,1)} %param.8), kind=kLoop, calls=%fused_computation.24 | loop fusion | bytes 6291456 | tf_op jit(solution)/shard_map/slice | solution.py:190
  168.0 2.2 %all-to-all-done.1 = bf16[8,1,6,16,128]{4,3,2,1,0:T(8,128)(2,1)S(1)} async-done(((bf16[8,1,6,16,128]{4,3,2,1,0:T(8,128)(2,1)}), bf16[8,1,6,16,128]{4,3,2,1,0:T(8,128)(2,1)S(1)}, u32[]{:S(2)}, u32[]{:S(2)}) %all-to-all-start.1) | async-done | bytes 196640 | tf_op jit(solution)/shard_map/all_to_all | solution.py:229
  170.2 0.1 reshape.76
  170.2 0.1 fusion.12
  170.4 0.5 fusion.4
  170.9 0.5 fusion.5
  171.5 0.6 fusion.9
  172.0 0.6 fusion.8
  172.6 0.8 copy.47
  173.4 1.6 bitcast_reduce_fusion
  175.0 1.0 reshape.89
  176.0 0.0 reduce-scatter.4.cloned.1.call-update
  176.0 17.2 %reduce-scatter.4.cloned.1.call-done = f32[32,16]{1,0:T(8,128)} async-done(((f32[128,16]{1,0:T(8,128)}), f32[32,16]{1,0:T(8,128)}) %reduce-scatter.4.cloned.1.call-update) | async-done | bytes 2064
  193.2 1.1 reshape.90
  194.3 0.8 copy.48
  (6 shorter events, 0.0 us)
Async XLA Ops:
  6.5 3.7 %copy-start = (s32[4,2]{0,1:T(2,128)S(1)}, s32[4,2]{0,1:T(2,128)}, u32[]{:S(2)}) copy-start(s32[4,2]{0,1:T(2,128)} %param.10) | copy-start | bytes 100
  6.5 66.1 %all-gather.5.cloned.1.call-start = ((), (), s32[]{:S(2)}) async-start(), calls=%async_computation.4 | async-start | bytes 3244032 | tf_op jit(solution)/shard_map/all_gather | solution.py:211
  7.5 12.2 %copy-start.2 = (s32[4]{0:T(128)S(1)}, s32[4]{0:T(128)}, u32[]{:S(2)}) copy-start(s32[4]{0:T(128)} %param.9) | copy-start | bytes 52
  8.2 13.6 %copy-start.1 = (f32[4,2]{0,1:T(2,128)S(1)}, f32[4,2]{0,1:T(2,128)}, u32[]{:S(2)}) copy-start(f32[4,2]{0,1:T(2,128)} %param.11) | copy-start | bytes 100
  8.2 138.1 %all-gather.3.cloned.1.call-start = ((), (), s32[]{:S(2)}) async-start(), calls=%async_computation.3 | async-start | bytes 7299072 | tf_op jit(solution)/shard_map/all_gather | solution.py:211
  14.5 12.1 %all-to-all-start = ((bf16[8,1,6,16,128]{4,3,2,1,0:T(8,128)(2,1)}), bf16[8,1,6,16,128]{4,3,2,1,0:T(8,128)(2,1)S(1)}, u32[]{:S(2)}, u32[]{:S(2)}) async-start(bf16[8,1,6,16,128]{4,3,2,1,0:T(8,128)(2,1)} %reshape.75), calls=%async_computation | async-start | bytes 393216 | tf_op jit(solution)/shard_map/all_to_all | solution.py:221
  160.6 9.5 %all-to-all-start.1 = ((bf16[8,1,6,16,128]{4,3,2,1,0:T(8,128)(2,1)}), bf16[8,1,6,16,128]{4,3,2,1,0:T(8,128)(2,1)S(1)}, u32[]{:S(2)}, u32[]{:S(2)}) async-start(bf16[8,1,6,16,128]{4,3,2,1,0:T(8,128)(2,1)} %bitcast.74), calls=%async_computation.1 | async-start | bytes 393216 | tf_op jit(solution)/shard_map/all_to_all | solution.py:229
  164.0 29.1 %reduce-scatter.4.cloned.1.call-start = ((), (), s32[]{:S(2)}) async-start(), calls=%async_computation.5 | async-start | bytes 81920
Sparse Core Ops, SparseCore 0:
  10.2 62.3 all-gather.4
  75.4 70.8 all-gather.2
  176.1 16.9 reduce-scatter.3

commit v2 on v1

--- a/solution.py
+++ b/solution.py
@@ -8,6 +8,7 @@
 from jax.sharding import PartitionSpec as P
 
 LANES = 128
+MESH = pl.DeviceIdType.MESH
 
 
 def roll(x, by, axis):
@@ -47,8 +48,151 @@
     return up, down
 
 
+def spread_kernel(n_time, blocks, held, start_ref, gauge_ref, time_ref, picked_ref, gauge_all, time_all,
+                  source_all, arrived, chosen, settled, send_sem, recv_sem, self_sem,
+                  pick_send, pick_recv, source_send, source_recv):
+    t, z = lax.axis_index("tm"), lax.axis_index("space")
+    chip, core = t // 2, lax.rem(t, 2)
+    chips = n_time // 2
+    partner = t + 1 - 2 * core
+
+    barrier = pltpu.get_barrier_semaphore()
+    for k in range(1, n_time):
+        pl.semaphore_signal(barrier, inc=1, device_id={"tm": lax.rem(t + k, n_time)}, device_id_type=MESH)
+    for k in range(1, blocks):
+        pl.semaphore_signal(barrier, inc=1, device_id={"space": lax.rem(z + k, blocks)}, device_id_type=MESH)
+    pl.semaphore_wait(barrier, n_time + blocks - 2)
+
+    pending = []
+
+    def send(src, dst, send_at, recv_at, target):
+        copy = pltpu.make_async_remote_copy(src_ref=src, dst_ref=dst, send_sem=send_at, recv_sem=recv_at,
+                                            device_id=target, device_id_type=MESH)
+        copy.start()
+        pending.append(copy)
+
+    count = [0]
+
+    def send_block(block, target, own=False):
+        for kind, (mine, whole) in enumerate(((gauge_ref, gauge_all), (time_ref, time_all))):
+            send(mine if own else whole.at[block], whole.at[block], send_sem.at[kind, count[0]],
+                 recv_sem.at[kind, block], target)
+        count[0] += 1
+
+    def await_block(block):
+        for kind, whole in enumerate((gauge_all, time_all)):
+            pltpu.make_async_copy(whole.at[block], whole.at[block], recv_sem.at[kind, block]).wait()
+
+    def at(k, of_chip, of_core):
+        return (of_chip * 2 + of_core) * blocks + lax.rem(z + k, blocks)
+
+    own = at(0, chip, core)
+    square = chips == 4
+    if square:
+        low, high = lax.rem(chip, 2), chip // 2
+        across = chip + 1 - 2 * low
+        along = chip + 2 - 4 * high
+        corner = 3 - chip
+        near = [across, along]
+    else:
+        near = [lax.rem(chip + k, chips) for k in range(1, chips)]
+
+    def to_chip(of_chip):
+        return {"tm": of_chip * 2 + core}
+
+    for k in range(1, blocks):
+        send_block(own, {"space": lax.rem(z + k, blocks)}, True)
+    for of_chip in near:
+        send_block(own, to_chip(of_chip), True)
+    locals_ = [pltpu.make_async_copy(gauge_ref, gauge_all.at[own], self_sem.at[0]),
+               pltpu.make_async_copy(time_ref, time_all.at[own], self_sem.at[1]),
+               pltpu.make_async_copy(picked_ref.at[t], arrived.at[t], self_sem.at[2])]
+    for copy in locals_:
+        copy.start()
+    for k in range(1, n_time):
+        to = lax.rem(t + k, n_time)
+        send(picked_ref.at[to], arrived.at[t], pick_send.at[k], pick_recv.at[t], {"tm": to})
+    send_block(own, {"tm": partner}, True)
+
+    for copy in locals_:
+        copy.wait()
+    for k in range(1, n_time):
+        frm = lax.rem(t + k, n_time)
+        pltpu.make_async_copy(arrived.at[frm], arrived.at[frm], pick_recv.at[frm]).wait()
+    for v in range(held):
+        total = jnp.zeros(arrived.shape[2:], jnp.float32)
+        for s in range(n_time):
+            flag = jnp.where(start_ref[v] == s, 1.0, 0.0).astype(jnp.float32)
+            total = total + flag * arrived[s, v].astype(jnp.float32)
+        chosen[v] = total.astype(jnp.bfloat16)
+    copy = pltpu.make_async_copy(chosen, settled, self_sem.at[3])
+    copy.start()
+    copy.wait()
+    copy = pltpu.make_async_copy(settled, source_all.at[z], self_sem.at[4])
+    copy.start()
+    for k in range(1, blocks):
+        send(settled, source_all.at[z], source_send.at[k], source_recv.at[z],
+             {"space": lax.rem(z + k, blocks)})
+    copy.wait()
+
+    order = sorted(range(blocks), key=lambda k: (min(k, blocks - k), k))
+    for k in order:
+        if k > 0:
+            block = at(k, chip, core)
+            await_block(block)
+            for of_chip in near:
+                send_block(block, to_chip(of_chip))
+            send_block(block, {"tm": partner})
+        for place, of_chip in enumerate(near):
+            block = at(k, of_chip, core)
+            await_block(block)
+            if square and k % 2 == place:
+                send_block(block, to_chip(near[1 - place]))
+            send_block(block, {"tm": partner})
+    if square:
+        for k in order:
+            block = at(k, corner, core)
+            await_block(block)
+            send_block(block, {"tm": partner})
+    for of_chip in range(chips):
+        for k in range(blocks):
+            await_block(at(k, of_chip, 1 - core))
+    for k in range(1, blocks):
+        frm = lax.rem(z + k, blocks)
+        pltpu.make_async_copy(source_all.at[frm], source_all.at[frm], source_recv.at[frm]).wait()
+    for copy in pending:
+        copy.wait_send()
+
+
+def spread(gauge, time, picked, starts, n_time, blocks):
+    held = picked.shape[1]
+    n = n_time * blocks
+    vmem = pl.BlockSpec(memory_space=pltpu.VMEM)
+    anywhere = pl.BlockSpec(memory_space=pl.ANY)
+    dma = pltpu.SemaphoreType.DMA
+    return pl.pallas_call(
+        lambda *refs: spread_kernel(n_time, blocks, held, *refs),
+        out_shape=[
+            jax.ShapeDtypeStruct((n,) + gauge.shape, gauge.dtype),
+            jax.ShapeDtypeStruct((n,) + time.shape, time.dtype),
+            jax.ShapeDtypeStruct((blocks,) + picked.shape[1:], picked.dtype),
+        ],
+        in_specs=[pl.BlockSpec(memory_space=pltpu.SMEM), vmem, vmem, vmem],
+        out_specs=[anywhere] * 3,
+        scratch_shapes=[
+            pltpu.VMEM(picked.shape, picked.dtype),
+            pltpu.VMEM(picked.shape[1:], picked.dtype),
+            pltpu.VMEM(picked.shape[1:], picked.dtype),
+            dma((2, n + blocks + n)), dma((2, n)), dma((5,)),
+            dma((n_time,)), dma((n_time,)), dma((blocks,)), dma((blocks,)),
+        ],
+        compiler_params=pltpu.CompilerParams(collective_id=0, has_side_effects=True),
+        name="spread",
+    )(starts, gauge, time, picked)
+
+
 def evolve_kernel(planes, rows, blocks, side, start_ref, place_ref, weight_ref, gauge_ref, time_ref,
-                  source_ref, out_ref, field, turned):
+                  source_ref, out_ref, field, turned, wide):
     which, rounds = pl.program_id(0), pl.program_id(1)
     extent = planes * blocks
     weight = weight_ref[which]
@@ -71,10 +215,31 @@
 
     def gauge(block, direction):
         def link(part, row, column):
-            at = ((part * 3 + direction) * 3 + row) * 3 + column
-            value = gauge_ref[0, block, at].astype(jnp.float32)
-            return value.reshape(planes, rows, LANES)
+            return wide[block, ((part * 3 + direction) * 3 + row) * 3 + column]
         return link
+
+    def shaped(x):
+        return x.astype(jnp.float32).reshape(planes, rows, LANES)
+
+    def third_row(u):
+        real, imag = [], []
+        for c in range(3):
+            d, e = (c + 1) % 3, (c + 2) % 3
+            real.append(u[0][0][d] * u[0][1][e] - u[1][0][d] * u[1][1][e]
+                        - u[0][0][e] * u[0][1][d] + u[1][0][e] * u[1][1][d])
+            imag.append(u[0][0][e] * u[1][1][d] + u[1][0][e] * u[0][1][d]
+                        - u[0][0][d] * u[1][1][e] - u[1][0][d] * u[0][1][e])
+        return real, imag
+
+    def widen(block, nothing):
+        for direction in range(3):
+            u = [[[shaped(gauge_ref[0, block, ((part * 3 + direction) * 2 + row) * 3 + c])
+                   for c in range(3)] for row in range(2)] for part in range(2)]
+            for part, extra in enumerate(third_row(u)):
+                for row, values in enumerate(u[part] + [extra]):
+                    for c in range(3):
+                        wide[block, ((part * 3 + direction) * 3 + row) * 3 + c] = values[c]
+        return nothing
 
     def read(ref, first):
         return [[ref[part * 3 + c, pl.ds(first, planes)] for c in range(3)] for part in range(2)]
@@ -117,17 +282,10 @@
         close(dst)
 
     def through_time(block, vec):
-        u = [[[time_ref[0, block, (part * 2 + row) * 3 + c].reshape(planes, rows, LANES) for c in range(3)]
+        u = [[[shaped(time_ref[0, block, (part * 2 + row) * 3 + c]) for c in range(3)]
               for row in range(2)] for part in range(2)]
-        third = [[], []]
-        for c in range(3):
-            d, e = (c + 1) % 3, (c + 2) % 3
-            third[0].append(u[0][0][d] * u[0][1][e] - u[1][0][d] * u[1][1][e]
-                            - u[0][0][e] * u[0][1][d] + u[1][0][e] * u[1][1][d])
-            third[1].append(-(u[0][0][d] * u[1][1][e] + u[1][0][d] * u[0][1][e]
-                              - u[0][0][e] * u[1][1][d] - u[1][0][e] * u[0][1][d]))
-        u[0].append(third[0])
-        u[1].append(third[1])
+        for part, extra in enumerate(third_row(u)):
+            u[part].append(extra)
         real, imag = [], []
         for c in range(3):
             real.append(sum(u[0][row][c] * vec[0][row] + u[1][row][c] * vec[1][row] for row in range(3)))
@@ -142,6 +300,7 @@
                 field[at, pl.ds(block * planes, planes)] = value.reshape(planes, rows, LANES)
         close(field)
 
+    lax.fori_loop(0, blocks, widen, 0)
     hop(field, turned, through_time)
     hop(turned, field, lambda block, vec: vec)
     mine = place_ref[0] * planes
@@ -177,7 +336,8 @@
             out_specs=pl.BlockSpec(
                 (1, 1, 6, tile, LANES),
                 lambda v, r, start, place: (v, lax.rem(start[v] + r, n_time), 0, 0, 0)),
-            scratch_shapes=[pltpu.VMEM((6, extent + 1, rows, LANES), jnp.float32)] * 2,
+            scratch_shapes=[pltpu.VMEM((6, extent + 1, rows, LANES), jnp.float32)] * 2
+            + [pltpu.VMEM((blocks, 54, planes, rows, LANES), jnp.float32)],
         ),
         name="evolve",
     )(starts, place, weights, gauge_all, time_all, sources)
@@ -207,21 +367,16 @@
     coef_flat = jnp.pad(kinetic_coef.reshape(-1), fill)
     my_sinks = sink_vectors[0]
 
-    def gather(x):
-        whole = lax.all_gather(x, ("tm", "space"), axis=0, tiled=False)
-        return whole.reshape((n_time, blocks) + x.shape)
-
-    gauge_all = gather(gauge_links.astype(jnp.bfloat16).reshape(54, tile, LANES))
-    time_all = gather(time_links[0, :, :2].reshape(12, tile, LANES))
-
     mine = lambda x: lax.dynamic_slice_in_dim(x, my_time * held, held)
     starts = mine(start_flat)
+    gauge = gauge_links[0, :, :, :2].astype(jnp.bfloat16).reshape(36, tile, LANES)
+    time = time_links[0, :, :2].reshape(12, tile, LANES)
     picked = jnp.take(my_sinks, index_flat, axis=1)
     picked = jnp.moveaxis(picked, 1, 0).reshape(n_time, held, 6, tile, LANES)
-    sent = lax.all_to_all(picked, "tm", 0, 0, tiled=False)
-    chosen = jnp.stack([lax.dynamic_index_in_dim(sent[:, v], starts[v], 0, keepdims=False)
-                        for v in range(held)])
-    sources = jnp.moveaxis(lax.all_gather(chosen, "space", axis=0, tiled=False), 0, 1)
+    gauge_all, time_all, sources = spread(gauge, time, picked, starts, n_time, blocks)
+    gauge_all = gauge_all.reshape((n_time, blocks) + gauge.shape)
+    time_all = time_all.reshape((n_time, blocks) + time.shape)
+    sources = jnp.moveaxis(sources, 0, 1)
 
     evolve.planes = planes
     place = lax.axis_index("space").astype(jnp.int32)[None]

time: 202 us -> 142 us (0.70)
  waiting for transfers between devices: 128 us -> 22.8 us
  Pallas kernels: 14.3 us -> 79.7 us
  blocking collectives: 14.3 us -> 0 us
  starting transfers between devices: 8.67 us -> 3.43 us
    all_gather x2 -> x0, waiting for transfers between devices: 105 us -> none  [gather(): whole = lax.all_gather(x, ('tm', 'space'), axis=0, tiled=False)]
    pallas_call x0 -> x1, Pallas kernels: none -> 64.5 us  [spread(): pl.pallas_call(lambda *refs: spread_kernel(n_time, blocks, held, *refs),...]
    all_gather x1 -> x0, blocking collectives: 14.3 us -> none  [local(): lax.all_gather(chosen, 'space', axis=0, tiled=False)]
    all_to_all x1 -> x0, starting transfers between devices: 5.2 us -> none  [local(): sent = lax.all_to_all(picked, 'tm', 0, 0, tiled=False)]
    unnamed x4 -> x2, waiting for transfers between devices: 17.2 us -> 20.6 us
    all_to_all x1 -> x0, waiting for transfers between devices: 2.77 us -> none  [local(): sent = lax.all_to_all(picked, 'tm', 0, 0, tiled=False)]
    unnamed x13 -> x9, local copies, waits for them, and re-layouts: 5.49 us -> 6.17 us
  transfers between devices with their start and end apart: 5 -> 2, of which waited for: 5 -> 2; matrix products, arithmetic and copies ran while one was open for 6% -> 3% of each run, Pallas kernels for 0% -> 0%
where the time goes in v2:
time: 142 us; the launch traced here: 141 us
  Pallas kernels  79.7 us (56%)
  waiting for transfers between devices  22.8 us (16%)
  local copies, waits for them, and re-layouts  18.7 us (13%)
  between operations  14.1 us (10%)
  starting transfers between devices  3.43 us (2%)
  matrix products  2.2 us (2%)
    pallas_call x1, Pallas kernels, spread(): pl.pallas_call(lambda *refs: spread_kernel(n_time, blocks, held, *refs),...  64.5 us
    unnamed x2, waiting for transfers between devices  20.6 us
    pallas_call x1, Pallas kernels, evolve(): pl.pallas_call(kernel, out_shape=jax.ShapeDtypeStruct((held, n_time, 6, t...  15.2 us
    unnamed x9, local copies, waits for them, and re-layouts  6.17 us
    slice x2, local copies, waits for them, and re-layouts, project(): real_part = dot(sinks[0], rounded[:, 0]) + dot(sinks[1], rounded[:, 1])  4.02 us
    all_to_all x1, starting transfers between devices, local(): back = lax.all_to_all(jnp.moveaxis(evolved, 1, 0), 'tm', 0, 0, tiled=False)  3.39 us
  transfers between devices with their start and end apart: 2, of which 2 were waited for; matrix products, arithmetic and copies ran while one was open for 3% of the time, Pallas kernels for 0%

profile of v2, /device:TPU:0, one launch (start us, length us, event | category | flops | bytes accessed | tf_op | source)
XLA Modules:
  0.0 141.1 jit_solution(10602764989910174747)
XLA Ops:
  6.5 0.0 slice-start
  6.5 0.0 copy-start
  6.5 0.8 copy.34
  7.3 0.1 reshape.72
  7.4 0.1 reshape.71
  7.5 0.7 broadcast_in_dim.16
  8.2 0.1 reshape.69
  8.3 2.8 %gather_fusion = bf16[8,2,3,2,1024]{4,3,2,1,0:T(2,128)(2,1)S(1)} fusion(bf16[2,128,3,2,1024]{4,3,2,1,0:T(2,128)(2,1)} %bitcast.70, s32[1024]{0:T(1024)S(1)} %pad_clamp_fusion), kind=kCustom, calls=%fused_computation | custom fusion | bytes 393248 | tf_op jit(solution)/shard_map/jit(_take)/gather | solution.py:374
  11.2 0.2 broadcast_select_fusion
  11.4 0.8 reshape.73.refs_3_
  12.2 1.1 slice.37
  13.3 0.8 convert_element_type.5.refs_1_
  14.1 0.0 slice-done
  14.1 0.7 reshape_squeeze.3.refs_2_
  14.8 0.0 copy-done
  14.8 0.1 copy.33
  14.9 0.1 reshape.70
  15.0 0.6 dynamic_slice.6.refs_0_
  15.6 0.6 dynamic_slice.7
  16.8 64.5 %spread.1 = (bf16[32,36,16,128]{3,2,1,0:T(8,128)(2,1)}, f32[32,12,16,128]{3,2,1,0:T(8,128)}, bf16[4,1,6,16,128]{4,3,2,1,0:T(8,128)(2,1)}) custom-call(s32[1]{0:T(128)} %dynamic_slice.6.refs_0_, bf16[36,16,128]{2,1,0:T(8,128)(2,1)} %convert_element_type.5.refs_1_, f32[12,16,128]{2,1,0:T(8,128)} %reshape_squeeze.3.refs_2_, ...), custom_call_target="tpu_custom_call" | custom-call | tf_op jit(solution)/shard_map/spread/pallas_call | solution.py:173
  81.3 15.2 %evolve.1 = bf16[1,8,6,16,128]{4,3,2,1,0:T(8,128)(2,1)} custom-call(s32[1]{0:T(128)} %dynamic_slice.6.refs_0_, s32[1]{0:T(128)} %bitcast.refs_1_, f32[1]{0:T(128)S(6)} %mul.3.refs_2_, bf16[8,4,36,16,128]{4,3,2,1,0:T(8,128)(2,1)} %bitcast.69, f32[8,4,12,16,128]{4,3,2,1,0:T(8,128)} %bitcast.71, bf16[1,4,6,16,128]{4,3,2,1,0:T(8,128)(2,1)} %bitcast.74), custom_call_target="tpu_custom_call" | custom-call | tf_op jit(solution)/shard_map/evolve/pallas_call | solution.py:324
  96.5 3.4 %all-to-all-start = ((bf16[8,1,6,16,128]{4,3,2,1,0:T(8,128)(2,1)}), bf16[8,1,6,16,128]{4,3,2,1,0:T(8,128)(2,1)S(1)}, u32[]{:S(2)}, u32[]{:S(2)}) async-start(bf16[8,1,6,16,128]{4,3,2,1,0:T(8,128)(2,1)} %bitcast.73), calls=%async_computation | async-start | bytes 393216 | tf_op jit(solution)/shard_map/all_to_all | solution.py:384
  99.9 0.0 reduce-scatter.4.cloned.1.call-start
  99.9 3.9 %fusion.11 = (bf16[1,1,128,3,2,1024]{5,4,3,2,1,0:T(2,128)(2,1)S(1)}, bf16[1,1,128,3,2,1024]{5,4,3,2,1,0:T(2,128)(2,1)S(1)}) fusion(bf16[1,2,128,3,2,1024]{5,4,3,2,1,0:T(2,128)(2,1)} %param.8), kind=kLoop, calls=%fused_computation.24 | loop fusion | bytes 6291456 | tf_op jit(solution)/shard_map/slice | solution.py:350
  103.8 2.2 %all-to-all-done = bf16[8,1,6,16,128]{4,3,2,1,0:T(8,128)(2,1)S(1)} async-done(((bf16[8,1,6,16,128]{4,3,2,1,0:T(8,128)(2,1)}), bf16[8,1,6,16,128]{4,3,2,1,0:T(8,128)(2,1)S(1)}, u32[]{:S(2)}, u32[]{:S(2)}) %all-to-all-start) | async-done | bytes 196640 | tf_op jit(solution)/shard_map/all_to_all | solution.py:384
  106.0 0.1 reshape.76
  106.1 0.1 fusion.12
  106.2 0.5 fusion.4
  106.8 0.5 fusion.5
  107.3 0.6 fusion.9
  107.9 0.6 fusion.8
  108.4 0.8 copy.47
  109.2 1.6 %bitcast_reduce_fusion = f32[128,2,4,2]{3,2,1,0:T(4,128)S(1)} fusion(f32[2,4,2,1,128]{3,2,1,0,4:T(2,128)S(1)} %copy.47), kind=kLoop, calls=%fused_computation.13 | loop fusion | bytes 16384
  110.8 1.0 reshape.89
  111.8 0.0 reduce-scatter.4.cloned.1.call-update
  111.8 20.5 %reduce-scatter.4.cloned.1.call-done = f32[32,16]{1,0:T(8,128)} async-done(((f32[128,16]{1,0:T(8,128)}), f32[32,16]{1,0:T(8,128)}) %reduce-scatter.4.cloned.1.call-update) | async-done | bytes 2064
  132.4 1.1 reshape.90
  133.5 0.8 copy.48
  (4 shorter events, 0.0 us)
Async XLA Ops:
  6.5 7.5 %slice-start = ((f32[1,2,3,3,2,1024]{5,4,3,2,1,0:T(2,128)}), f32[1,2,2,3,2,1024]{5,4,3,2,1,0:T(2,128)S(1)}, s32[]{:S(2)}) async-start(f32[1,2,3,3,2,1024]{5,4,3,2,1,0:T(2,128)} %param.7), calls=%async_computation.3 | async-start | bytes 196608 | tf_op jit(solution)/shard_map/slice | solution.py:373
  6.5 8.3 %copy-start = (f32[4,2]{0,1:T(2,128)S(1)}, f32[4,2]{0,1:T(2,128)}, u32[]{:S(2)}) copy-start(f32[4,2]{0,1:T(2,128)} %param.11) | copy-start | bytes 100
  96.5 9.5 %all-to-all-start = ((bf16[8,1,6,16,128]{4,3,2,1,0:T(8,128)(2,1)}), bf16[8,1,6,16,128]{4,3,2,1,0:T(8,128)(2,1)S(1)}, u32[]{:S(2)}, u32[]{:S(2)}) async-start(bf16[8,1,6,16,128]{4,3,2,1,0:T(8,128)(2,1)} %bitcast.73), calls=%async_computation | async-start | bytes 393216 | tf_op jit(solution)/shard_map/all_to_all | solution.py:384
  99.9 32.5 %reduce-scatter.4.cloned.1.call-start = ((), (), s32[]{:S(2)}) async-start(), calls=%async_computation.2 | async-start | bytes 81920
Sparse Core Ops, SparseCore 0:
  112.0 20.3 reduce-scatter.3

commit v3 on v2

--- a/solution.py
+++ b/solution.py
@@ -65,28 +65,39 @@
 
     pending = []
 
-    def send(src, dst, send_at, recv_at, target):
+    def when(condition, action):
+        if condition is None:
+            action()
+        else:
+            pl.when(condition)(action)
+
+    def both(first, second):
+        return second if first is None else first if second is None else jnp.logical_and(first, second)
+
+    def send(src, dst, send_at, recv_at, target, condition=None):
         copy = pltpu.make_async_remote_copy(src_ref=src, dst_ref=dst, send_sem=send_at, recv_sem=recv_at,
                                             device_id=target, device_id_type=MESH)
-        copy.start()
-        pending.append(copy)
+        when(condition, copy.start)
+        pending.append((condition, copy))
 
     count = [0]
 
-    def send_block(block, target, own=False):
+    def send_block(block, target, condition=None, own=False):
         for kind, (mine, whole) in enumerate(((gauge_ref, gauge_all), (time_ref, time_all))):
             send(mine if own else whole.at[block], whole.at[block], send_sem.at[kind, count[0]],
-                 recv_sem.at[kind, block], target)
+                 recv_sem.at[kind, block], target, condition)
         count[0] += 1
 
-    def await_block(block):
-        for kind, whole in enumerate((gauge_all, time_all)):
-            pltpu.make_async_copy(whole.at[block], whole.at[block], recv_sem.at[kind, block]).wait()
-
-    def at(k, of_chip, of_core):
-        return (of_chip * 2 + of_core) * blocks + lax.rem(z + k, blocks)
-
-    own = at(0, chip, core)
+    def await_block(block, condition=None):
+        def wait():
+            for kind, whole in enumerate((gauge_all, time_all)):
+                pltpu.make_async_copy(whole.at[block], whole.at[block], recv_sem.at[kind, block]).wait()
+        when(condition, wait)
+
+    def at(depth, of_chip, of_core):
+        return (of_chip * 2 + of_core) * blocks + depth
+
+    own = at(z, chip, core)
     square = chips == 4
     if square:
         low, high = lax.rem(chip, 2), chip // 2
@@ -100,68 +111,86 @@
     def to_chip(of_chip):
         return {"tm": of_chip * 2 + core}
 
-    for k in range(1, blocks):
-        send_block(own, {"space": lax.rem(z + k, blocks)}, True)
+    below = (z > 0, {"space": lax.rem(z + blocks - 1, blocks)})
+    above = (z < blocks - 1, {"space": lax.rem(z + 1, blocks)})
+    for condition, target in (below, above):
+        send_block(own, target, condition, True)
+    for k in range(1, n_time):
+        to = lax.rem(t + k, n_time)
+        send(picked_ref.at[to], arrived.at[t], pick_send.at[k], pick_recv.at[t], {"tm": to})
     for of_chip in near:
-        send_block(own, to_chip(of_chip), True)
+        send_block(own, to_chip(of_chip), None, True)
+    send_block(own, {"tm": partner}, None, True)
     locals_ = [pltpu.make_async_copy(gauge_ref, gauge_all.at[own], self_sem.at[0]),
                pltpu.make_async_copy(time_ref, time_all.at[own], self_sem.at[1]),
                pltpu.make_async_copy(picked_ref.at[t], arrived.at[t], self_sem.at[2])]
     for copy in locals_:
         copy.start()
-    for k in range(1, n_time):
-        to = lax.rem(t + k, n_time)
-        send(picked_ref.at[to], arrived.at[t], pick_send.at[k], pick_recv.at[t], {"tm": to})
-    send_block(own, {"tm": partner}, True)
-
-    for copy in locals_:
+    def settle():
+        for copy in locals_:
+            copy.wait()
+        for k in range(1, n_time):
+            frm = lax.rem(t + k, n_time)
+            pltpu.make_async_copy(arrived.at[frm], arrived.at[frm], pick_recv.at[frm]).wait()
+        for v in range(held):
+            total = jnp.zeros(arrived.shape[2:], jnp.float32)
+            for s in range(n_time):
+                flag = jnp.where(start_ref[v] == s, 1.0, 0.0).astype(jnp.float32)
+                total = total + flag * arrived[s, v].astype(jnp.float32)
+            chosen[v] = total.astype(jnp.bfloat16)
+        copy = pltpu.make_async_copy(chosen, settled, self_sem.at[3])
+        copy.start()
         copy.wait()
-    for k in range(1, n_time):
-        frm = lax.rem(t + k, n_time)
-        pltpu.make_async_copy(arrived.at[frm], arrived.at[frm], pick_recv.at[frm]).wait()
-    for v in range(held):
-        total = jnp.zeros(arrived.shape[2:], jnp.float32)
-        for s in range(n_time):
-            flag = jnp.where(start_ref[v] == s, 1.0, 0.0).astype(jnp.float32)
-            total = total + flag * arrived[s, v].astype(jnp.float32)
-        chosen[v] = total.astype(jnp.bfloat16)
-    copy = pltpu.make_async_copy(chosen, settled, self_sem.at[3])
-    copy.start()
-    copy.wait()
-    copy = pltpu.make_async_copy(settled, source_all.at[z], self_sem.at[4])
-    copy.start()
-    for k in range(1, blocks):
-        send(settled, source_all.at[z], source_send.at[k], source_recv.at[z],
-             {"space": lax.rem(z + k, blocks)})
-    copy.wait()
-
-    order = sorted(range(blocks), key=lambda k: (min(k, blocks - k), k))
-    for k in order:
-        if k > 0:
-            block = at(k, chip, core)
-            await_block(block)
-            for of_chip in near:
-                send_block(block, to_chip(of_chip))
-            send_block(block, {"tm": partner})
+        copy = pltpu.make_async_copy(settled, source_all.at[z], self_sem.at[4])
+        copy.start()
+        for k in range(1, blocks):
+            send(settled, source_all.at[z], source_send.at[k], source_recv.at[z],
+                 {"space": lax.rem(z + k, blocks)})
+        copy.wait()
+
+    items = [(0, None, z, None)]
+    for step in range(1, blocks):
+        items.append((step, z >= step, lax.rem(z + blocks - step, blocks), above))
+        items.append((step, z + step < blocks, lax.rem(z + step, blocks), below))
+
+    def from_column(item):
+        step, condition, depth, onward = item
+        block = at(depth, chip, core)
+        await_block(block, condition)
+        send_block(block, onward[1], both(condition, onward[0]))
+        for of_chip in near:
+            send_block(block, to_chip(of_chip), condition)
+        send_block(block, {"tm": partner}, condition)
+
+    def from_near(item):
+        step, condition, depth, onward = item
         for place, of_chip in enumerate(near):
-            block = at(k, of_chip, core)
-            await_block(block)
-            if square and k % 2 == place:
-                send_block(block, to_chip(near[1 - place]))
-            send_block(block, {"tm": partner})
+            block = at(depth, of_chip, core)
+            await_block(block, condition)
+            if square and step % 2 == place:
+                send_block(block, to_chip(near[1 - place]), condition)
+            send_block(block, {"tm": partner}, condition)
+
+    for place, item in enumerate(items):
+        if place > 0:
+            from_column(item)
+            from_near(items[place - 1])
+        if place == min(2, len(items) - 1):
+            settle()
+    from_near(items[-1])
     if square:
-        for k in order:
-            block = at(k, corner, core)
-            await_block(block)
-            send_block(block, {"tm": partner})
+        for step, condition, depth, onward in items:
+            block = at(depth, corner, core)
+            await_block(block, condition)
+            send_block(block, {"tm": partner}, condition)
     for of_chip in range(chips):
-        for k in range(blocks):
-            await_block(at(k, of_chip, 1 - core))
+        for depth in range(blocks):
+            await_block(at(depth, of_chip, 1 - core))
     for k in range(1, blocks):
         frm = lax.rem(z + k, blocks)
         pltpu.make_async_copy(source_all.at[frm], source_all.at[frm], source_recv.at[frm]).wait()
-    for copy in pending:
-        copy.wait_send()
+    for condition, copy in pending:
+        when(condition, copy.wait_send)
 
 
 def spread(gauge, time, picked, starts, n_time, blocks):
@@ -183,7 +212,7 @@
             pltpu.VMEM(picked.shape, picked.dtype),
             pltpu.VMEM(picked.shape[1:], picked.dtype),
             pltpu.VMEM(picked.shape[1:], picked.dtype),
-            dma((2, n + blocks + n)), dma((2, n)), dma((5,)),
+            dma((2, 4 * n + 8)), dma((2, n)), dma((5,)),
             dma((n_time,)), dma((n_time,)), dma((blocks,)), dma((blocks,)),
         ],
         compiler_params=pltpu.CompilerParams(collective_id=0, has_side_effects=True),
@@ -343,6 +372,52 @@
     )(starts, place, weights, gauge_all, time_all, sources)
 
 
+def collect_kernel(blocks, part_ref, out_ref, parts, send_sem, recv_sem, self_sem):
+    z = lax.axis_index("space")
+    barrier = pltpu.get_barrier_semaphore()
+    others = [lax.rem(z + k, blocks) for k in range(1, blocks)]
+    for other in others:
+        pl.semaphore_signal(barrier, inc=1, device_id={"space": other}, device_id_type=MESH)
+    pl.semaphore_wait(barrier, blocks - 1)
+    copies = []
+    for k, other in enumerate(others):
+        copies.append(pltpu.make_async_remote_copy(
+            src_ref=part_ref, dst_ref=parts.at[z], send_sem=send_sem.at[k], recv_sem=recv_sem.at[z],
+            device_id={"space": other}, device_id_type=MESH))
+        copies[-1].start()
+    mine = pltpu.make_async_copy(part_ref, parts.at[z], self_sem)
+    mine.start()
+    mine.wait()
+    for other in others:
+        pltpu.make_async_copy(parts.at[other], parts.at[other], recv_sem.at[other]).wait()
+    for copy in copies:
+        copy.wait_send()
+    total = parts[0]
+    for block in range(1, blocks):
+        total = total + parts[block]
+    width = out_ref.shape[1]
+    kept = total[:, :width]
+    for block in range(1, blocks):
+        kept = jnp.where(z == block, total[:, block * width:(block + 1) * width], kept)
+    out_ref[...] = kept
+
+
+def collect(partial, blocks):
+    rows, columns = partial.shape
+    vmem = pl.BlockSpec(memory_space=pltpu.VMEM)
+    dma = pltpu.SemaphoreType.DMA
+    return pl.pallas_call(
+        lambda *refs: collect_kernel(blocks, *refs),
+        out_shape=jax.ShapeDtypeStruct((rows, columns // blocks), jnp.float32),
+        in_specs=[vmem],
+        out_specs=vmem,
+        scratch_shapes=[pltpu.VMEM((blocks, rows, columns), jnp.float32),
+                        dma((blocks,)), dma((blocks,)), dma],
+        compiler_params=pltpu.CompilerParams(collective_id=1, has_side_effects=True),
+        name="collect",
+    )(partial)
+
+
 def project(sinks, rounded):
     def dot(a, b):
         return jnp.einsum("ecxs,vcxs->ve", a, b, preferred_element_type=jnp.float32)
@@ -384,8 +459,8 @@
     back = lax.all_to_all(jnp.moveaxis(evolved, 1, 0), "tm", 0, 0, tiled=False)
     rounded = back.reshape(n_time * held, 2, 3, planes, sites)[:count]
     correlations = project(my_sinks, rounded)
-    correlations = correlations.reshape(2, groups, per_group, 1, my_sinks.shape[1])
-    return lax.psum_scatter(correlations, "space", scatter_dimension=4, tiled=True)
+    total = collect(correlations.reshape(2 * count, -1), blocks)
+    return total.reshape(2, groups, per_group, 1, -1)
 
 
 def solution(mesh):

time: 142 us -> 107 us (0.75)
  waiting for transfers between devices: 22.8 us -> 2.25 us
  between operations: 14.1 us -> 0.7 us
  local copies, waits for them, and re-layouts: 18.7 us -> 14.7 us
  Pallas kernels: 79.7 us -> 82 us
    unnamed x2 -> x0, waiting for transfers between devices: 20.6 us -> none
    pallas_call x0 -> x1, Pallas kernels: none -> 7.1 us  [collect(): pl.pallas_call(lambda *refs: collect_kernel(blocks, *refs), out_shape=jax...]
    pallas_call x1, Pallas kernels: 64.5 us -> 59.7 us  [spread(): pl.pallas_call(lambda *refs: spread_kernel(n_time, blocks, held, *refs),...]
    unnamed x9 -> x5, local copies, waits for them, and re-layouts: 6.17 us -> 2.19 us
  transfers between devices with their start and end apart: 2 -> 1, of which waited for: 2 -> 1; matrix products, arithmetic and copies ran while one was open for 3% -> 4% of each run, Pallas kernels for 0% -> 0%
where the time goes in v3:
time: 107 us; the launch traced here: 106 us
  Pallas kernels  82 us (77%)
  local copies, waits for them, and re-layouts  14.7 us (14%)
  starting transfers between devices  3.39 us (3%)
  waiting for transfers between devices  2.25 us (2%)
  matrix products  2.2 us (2%)
    pallas_call x1, Pallas kernels, spread(): pl.pallas_call(lambda *refs: spread_kernel(n_time, blocks, held, *refs),...  59.7 us
    pallas_call x1, Pallas kernels, evolve(): pl.pallas_call(kernel, out_shape=jax.ShapeDtypeStruct((held, n_time, 6, t...  15.2 us
    pallas_call x1, Pallas kernels, collect(): pl.pallas_call(lambda *refs: collect_kernel(blocks, *refs), out_shape=jax...  7.1 us
    slice x2, local copies, waits for them, and re-layouts, project(): real_part = dot(sinks[0], rounded[:, 0]) + dot(sinks[1], rounded[:, 1])  4.02 us
    all_to_all x1, starting transfers between devices, local(): back = lax.all_to_all(jnp.moveaxis(evolved, 1, 0), 'tm', 0, 0, tiled=False)  3.39 us
    gather x1, local copies, waits for them, and re-layouts, local(): picked = jnp.take(my_sinks, index_flat, axis=1)  2.83 us
    all_to_all x1, waiting for transfers between devices, local(): back = lax.all_to_all(jnp.moveaxis(evolved, 1, 0), 'tm', 0, 0, tiled=False)  2.25 us
    dot_general x4, matrix products, dot(): return jnp.einsum('ecxs,vcxs->ve', a, b, preferred_element_type=jnp.float32)  2.2 us
  transfers between devices with their start and end apart: 1, of which 1 were waited for; matrix products, arithmetic and copies ran while one was open for 4% of the time, Pallas kernels for 0%

profile of v3, /device:TPU:0, one launch (start us, length us, event | category | flops | bytes accessed | tf_op | source)
XLA Modules:
  0.0 106.1 jit_solution(425506346796289802)
XLA Ops:
  0.0 0.0 slice-start
  0.0 0.0 copy-start
  0.0 0.8 copy.31
  0.8 0.1 reshape.73
  0.9 0.1 reshape.72
  1.0 0.7 broadcast_in_dim.16
  1.7 0.1 reshape.70
  1.8 2.8 %gather_fusion = bf16[8,2,3,2,1024]{4,3,2,1,0:T(2,128)(2,1)S(1)} fusion(bf16[2,128,3,2,1024]{4,3,2,1,0:T(2,128)(2,1)} %bitcast.78, s32[1024]{0:T(1024)S(1)} %pad_clamp_fusion), kind=kCustom, calls=%fused_computation | custom fusion | bytes 393248 | tf_op jit(solution)/shard_map/jit(_take)/gather | solution.py:449
  4.7 0.2 broadcast_select_fusion
  4.9 0.8 reshape.74.refs_3_
  5.7 1.1 %slice.37 = bf16[1,2,3,2,3,2,1024]{6,5,4,3,2,1,0:T(2,128)(2,1)S(1)} slice(f32[1,2,3,3,3,2,1024]{6,5,4,3,2,1,0:T(2,128)} %param.6), slice={[0:1], [0:2], [0:3], [0:2], [0:3], [0:2], [0:1024]} | slice | bytes 294912 | tf_op jit(solution)/shard_map/slice | solution.py:447
  6.8 0.8 convert_element_type.5.refs_1_
  7.6 0.0 slice-done
  7.6 0.7 reshape_squeeze.3.refs_2_
  8.3 0.0 copy-done
  8.3 0.1 copy.30
  8.4 0.1 reshape.71
  8.5 0.6 dynamic_slice.6.refs_0_
  9.1 0.6 dynamic_slice.7
  10.3 59.7 %spread.1 = (bf16[32,36,16,128]{3,2,1,0:T(8,128)(2,1)}, f32[32,12,16,128]{3,2,1,0:T(8,128)}, bf16[4,1,6,16,128]{4,3,2,1,0:T(8,128)(2,1)}) custom-call(s32[1]{0:T(128)} %dynamic_slice.6.refs_0_, bf16[36,16,128]{2,1,0:T(8,128)(2,1)} %convert_element_type.5.refs_1_, f32[12,16,128]{2,1,0:T(8,128)} %reshape_squeeze.3.refs_2_, ...), custom_call_target="tpu_custom_call" | custom-call | tf_op jit(solution)/shard_map/spread/pallas_call | solution.py:202
  70.0 15.2 %evolve.1 = bf16[1,8,6,16,128]{4,3,2,1,0:T(8,128)(2,1)} custom-call(s32[1]{0:T(128)} %dynamic_slice.6.refs_0_, s32[1]{0:T(128)} %bitcast.refs_1_, f32[1]{0:T(128)S(6)} %mul.3.refs_2_, bf16[8,4,36,16,128]{4,3,2,1,0:T(8,128)(2,1)} %bitcast.77, f32[8,4,12,16,128]{4,3,2,1,0:T(8,128)} %bitcast.79, bf16[1,4,6,16,128]{4,3,2,1,0:T(8,128)(2,1)} %bitcast.81), custom_call_target="tpu_custom_call" | custom-call | tf_op jit(solution)/shard_map/evolve/pallas_call | solution.py:353
  85.2 3.4 %all-to-all-start = ((bf16[8,1,6,16,128]{4,3,2,1,0:T(8,128)(2,1)}), bf16[8,1,6,16,128]{4,3,2,1,0:T(8,128)(2,1)S(1)}, u32[]{:S(2)}, u32[]{:S(2)}) async-start(bf16[8,1,6,16,128]{4,3,2,1,0:T(8,128)(2,1)} %bitcast.80), calls=%async_computation | async-start | bytes 393216 | tf_op jit(solution)/shard_map/all_to_all | solution.py:459
  88.6 3.9 %fusion.13 = (bf16[1,1,128,3,2,1024]{5,4,3,2,1,0:T(2,128)(2,1)S(1)}, bf16[1,1,128,3,2,1024]{5,4,3,2,1,0:T(2,128)(2,1)S(1)}) fusion(bf16[1,2,128,3,2,1024]{5,4,3,2,1,0:T(2,128)(2,1)} %param.8), kind=kLoop, calls=%fused_computation.25 | loop fusion | bytes 6291456 | tf_op jit(solution)/shard_map/slice | solution.py:425
  92.5 2.2 %all-to-all-done = bf16[8,1,6,16,128]{4,3,2,1,0:T(8,128)(2,1)S(1)} async-done(((bf16[8,1,6,16,128]{4,3,2,1,0:T(8,128)(2,1)}), bf16[8,1,6,16,128]{4,3,2,1,0:T(8,128)(2,1)S(1)}, u32[]{:S(2)}, u32[]{:S(2)}) %all-to-all-start) | async-done | bytes 196640 | tf_op jit(solution)/shard_map/all_to_all | solution.py:459
  94.7 0.1 reshape.77
  94.8 0.1 fusion.14
  94.9 0.5 fusion.4
  95.5 0.5 fusion.5
  96.0 0.6 fusion.11
  96.6 0.6 fusion.9
  97.1 0.6 maximum_bitcast_fusion.refs_0_
  97.7 7.1 %collect.1 = f32[16,32]{1,0:T(8,128)} custom-call(f32[16,128]{1,0:T(8,128)} %maximum_bitcast_fusion.refs_0_), custom_call_target="tpu_custom_call" | custom-call | tf_op jit(solution)/shard_map/collect/pallas_call | solution.py:409
  104.8 1.3 %copy.76 = f32[2,4,2,1,32]{4,3,2,1,0:T(1,128)} copy(f32[2,4,2,1,32]{4,3,2,1,0:T(1,128)} %bitcast.82) | data formatting | bytes 4096
  (3 shorter events, 0.0 us)
Async XLA Ops:
  0.0 7.6 %slice-start = ((f32[1,2,3,3,2,1024]{5,4,3,2,1,0:T(2,128)}), f32[1,2,2,3,2,1024]{5,4,3,2,1,0:T(2,128)S(1)}, s32[]{:S(2)}) async-start(f32[1,2,3,3,2,1024]{5,4,3,2,1,0:T(2,128)} %param.7), calls=%async_computation.1 | async-start | bytes 196608 | tf_op jit(solution)/shard_map/slice | solution.py:448
  0.0 8.3 %copy-start = (f32[4,2]{0,1:T(2,128)S(1)}, f32[4,2]{0,1:T(2,128)}, u32[]{:S(2)}) copy-start(f32[4,2]{0,1:T(2,128)} %param.11) | copy-start | bytes 100
  85.2 9.5 %all-to-all-start = ((bf16[8,1,6,16,128]{4,3,2,1,0:T(8,128)(2,1)}), bf16[8,1,6,16,128]{4,3,2,1,0:T(8,128)(2,1)S(1)}, u32[]{:S(2)}, u32[]{:S(2)}) async-start(bf16[8,1,6,16,128]{4,3,2,1,0:T(8,128)(2,1)} %bitcast.80), calls=%async_computation | async-start | bytes 393216 | tf_op jit(solution)/shard_map/all_to_all | solution.py:459

commit v4 on v3

--- a/solution.py
+++ b/solution.py
@@ -9,6 +9,7 @@
 
 LANES = 128
 MESH = pl.DeviceIdType.MESH
+VMEM_ROOM = 24 * 1024 * 1024
 
 
 def roll(x, by, axis):
@@ -197,7 +198,8 @@
     held = picked.shape[1]
     n = n_time * blocks
     vmem = pl.BlockSpec(memory_space=pltpu.VMEM)
-    anywhere = pl.BlockSpec(memory_space=pl.ANY)
+    size = n * (2 * math.prod(gauge.shape) + 4 * math.prod(time.shape))
+    landing = vmem if size <= VMEM_ROOM else pl.BlockSpec(memory_space=pl.ANY)
     dma = pltpu.SemaphoreType.DMA
     return pl.pallas_call(
         lambda *refs: spread_kernel(n_time, blocks, held, *refs),
@@ -207,7 +209,7 @@
             jax.ShapeDtypeStruct((blocks,) + picked.shape[1:], picked.dtype),
         ],
         in_specs=[pl.BlockSpec(memory_space=pltpu.SMEM), vmem, vmem, vmem],
-        out_specs=[anywhere] * 3,
+        out_specs=[landing] * 3,
         scratch_shapes=[
             pltpu.VMEM(picked.shape, picked.dtype),
             pltpu.VMEM(picked.shape[1:], picked.dtype),

time: 107 us -> 108 us (level)
  Pallas kernels: 82 us -> 83.4 us
    pallas_call x1, Pallas kernels: 59.7 us -> 61.1 us  [spread(): pl.pallas_call(lambda *refs: spread_kernel(n_time, blocks, held, *refs),...]
where the time goes in v4:
time: 108 us
  Pallas kernels  83.4 us (77%)
  local copies, waits for them, and re-layouts  14.7 us (14%)
  starting transfers between devices  3.39 us (3%)
  waiting for transfers between devices  2.25 us (2%)
  matrix products  2.2 us (2%)
    pallas_call x1, Pallas kernels, spread(): pl.pallas_call(lambda *refs: spread_kernel(n_time, blocks, held, *refs),...  61.1 us
    pallas_call x1, Pallas kernels, evolve(): pl.pallas_call(kernel, out_shape=jax.ShapeDtypeStruct((held, n_time, 6, t...  15.2 us
    pallas_call x1, Pallas kernels, collect(): pl.pallas_call(lambda *refs: collect_kernel(blocks, *refs), out_shape=jax...  7.1 us
    slice x2, local copies, waits for them, and re-layouts, project(): real_part = dot(sinks[0], rounded[:, 0]) + dot(sinks[1], rounded[:, 1])  4.02 us
    all_to_all x1, starting transfers between devices, local(): back = lax.all_to_all(jnp.moveaxis(evolved, 1, 0), 'tm', 0, 0, tiled=False)  3.39 us
    gather x1, local copies, waits for them, and re-layouts, local(): picked = jnp.take(my_sinks, index_flat, axis=1)  2.83 us
    all_to_all x1, waiting for transfers between devices, local(): back = lax.all_to_all(jnp.moveaxis(evolved, 1, 0), 'tm', 0, 0, tiled=False)  2.25 us
    dot_general x4, matrix products, dot(): return jnp.einsum('ecxs,vcxs->ve', a, b, preferred_element_type=jnp.float32)  2.2 us
  transfers between devices with their start and end apart: 1, of which 1 were waited for; matrix products, arithmetic and copies ran while one was open for 4% of the time, Pallas kernels for 0%

profile of v4, /device:TPU:0, one launch (start us, length us, event | category | flops | bytes accessed | tf_op | source)
XLA Modules:
  0.0 107.6 jit_solution(13988582230150452910)
XLA Ops:
  0.0 0.0 slice-start
  0.0 0.0 copy-start
  0.0 0.8 copy.31
  0.8 0.1 reshape.73
  0.9 0.1 reshape.72
  1.0 0.7 broadcast_in_dim.16
  1.7 0.1 reshape.70
  1.8 2.8 %gather_fusion = bf16[8,2,3,2,1024]{4,3,2,1,0:T(2,128)(2,1)S(1)} fusion(bf16[2,128,3,2,1024]{4,3,2,1,0:T(2,128)(2,1)} %bitcast.78, s32[1024]{0:T(1024)S(1)} %pad_clamp_fusion), kind=kCustom, calls=%fused_computation | custom fusion | bytes 393248 | tf_op jit(solution)/shard_map/jit(_take)/gather | solution.py:451
  4.7 0.2 broadcast_select_fusion
  4.9 0.8 reshape.74.refs_3_
  5.7 1.1 slice.37
  6.8 0.8 convert_element_type.5.refs_1_
  7.6 0.0 slice-done
  7.6 0.7 reshape_squeeze.3.refs_2_
  8.3 0.0 copy-done
  8.3 0.1 copy.30
  8.4 0.1 reshape.71
  8.5 0.6 dynamic_slice.6.refs_0_
  9.1 0.6 dynamic_slice.7
  10.3 61.1 %spread.1 = (bf16[32,36,16,128]{3,2,1,0:T(8,128)(2,1)}, f32[32,12,16,128]{3,2,1,0:T(8,128)}, bf16[4,1,6,16,128]{4,3,2,1,0:T(8,128)(2,1)}) custom-call(s32[1]{0:T(128)} %dynamic_slice.6.refs_0_, bf16[36,16,128]{2,1,0:T(8,128)(2,1)} %convert_element_type.5.refs_1_, f32[12,16,128]{2,1,0:T(8,128)} %reshape_squeeze.3.refs_2_, ...), custom_call_target="tpu_custom_call" | custom-call | tf_op jit(solution)/shard_map/spread/pallas_call | solution.py:204
  71.4 15.2 %evolve.1 = bf16[1,8,6,16,128]{4,3,2,1,0:T(8,128)(2,1)} custom-call(s32[1]{0:T(128)} %dynamic_slice.6.refs_0_, s32[1]{0:T(128)} %bitcast.refs_1_, f32[1]{0:T(128)S(6)} %mul.3.refs_2_, bf16[8,4,36,16,128]{4,3,2,1,0:T(8,128)(2,1)} %bitcast.77, f32[8,4,12,16,128]{4,3,2,1,0:T(8,128)} %bitcast.79, bf16[1,4,6,16,128]{4,3,2,1,0:T(8,128)(2,1)} %bitcast.81), custom_call_target="tpu_custom_call" | custom-call | tf_op jit(solution)/shard_map/evolve/pallas_call | solution.py:355
  86.6 3.4 %all-to-all-start = ((bf16[8,1,6,16,128]{4,3,2,1,0:T(8,128)(2,1)}), bf16[8,1,6,16,128]{4,3,2,1,0:T(8,128)(2,1)S(1)}, u32[]{:S(2)}, u32[]{:S(2)}) async-start(bf16[8,1,6,16,128]{4,3,2,1,0:T(8,128)(2,1)} %bitcast.80), calls=%async_computation | async-start | bytes 393216 | tf_op jit(solution)/shard_map/all_to_all | solution.py:461
  90.0 3.9 %fusion.13 = (bf16[1,1,128,3,2,1024]{5,4,3,2,1,0:T(2,128)(2,1)S(1)}, bf16[1,1,128,3,2,1024]{5,4,3,2,1,0:T(2,128)(2,1)S(1)}) fusion(bf16[1,2,128,3,2,1024]{5,4,3,2,1,0:T(2,128)(2,1)} %param.8), kind=kLoop, calls=%fused_computation.25 | loop fusion | bytes 6291456 | tf_op jit(solution)/shard_map/slice | solution.py:427
  93.9 2.2 %all-to-all-done = bf16[8,1,6,16,128]{4,3,2,1,0:T(8,128)(2,1)S(1)} async-done(((bf16[8,1,6,16,128]{4,3,2,1,0:T(8,128)(2,1)}), bf16[8,1,6,16,128]{4,3,2,1,0:T(8,128)(2,1)S(1)}, u32[]{:S(2)}, u32[]{:S(2)}) %all-to-all-start) | async-done | bytes 196640 | tf_op jit(solution)/shard_map/all_to_all | solution.py:461
  96.1 0.1 reshape.77
  96.2 0.1 fusion.14
  96.3 0.5 fusion.4
  96.9 0.5 fusion.5
  97.4 0.6 fusion.11
  98.0 0.6 fusion.9
  98.6 0.6 maximum_bitcast_fusion.refs_0_
  99.2 7.1 %collect.1 = f32[16,32]{1,0:T(8,128)} custom-call(f32[16,128]{1,0:T(8,128)} %maximum_bitcast_fusion.refs_0_), custom_call_target="tpu_custom_call" | custom-call | tf_op jit(solution)/shard_map/collect/pallas_call | solution.py:411
  106.3 1.3 %copy.76 = f32[2,4,2,1,32]{4,3,2,1,0:T(1,128)} copy(f32[2,4,2,1,32]{4,3,2,1,0:T(1,128)} %bitcast.82) | data formatting | bytes 4096
  (3 shorter events, 0.0 us)
Async XLA Ops:
  0.0 7.6 %slice-start = ((f32[1,2,3,3,2,1024]{5,4,3,2,1,0:T(2,128)}), f32[1,2,2,3,2,1024]{5,4,3,2,1,0:T(2,128)S(1)}, s32[]{:S(2)}) async-start(f32[1,2,3,3,2,1024]{5,4,3,2,1,0:T(2,128)} %param.7), calls=%async_computation.1 | async-start | bytes 196608 | tf_op jit(solution)/shard_map/slice | solution.py:450
  0.0 8.3 %copy-start = (f32[4,2]{0,1:T(2,128)S(1)}, f32[4,2]{0,1:T(2,128)}, u32[]{:S(2)}) copy-start(f32[4,2]{0,1:T(2,128)} %param.11) | copy-start | bytes 100
  86.6 9.5 %all-to-all-start = ((bf16[8,1,6,16,128]{4,3,2,1,0:T(8,128)(2,1)}), bf16[8,1,6,16,128]{4,3,2,1,0:T(8,128)(2,1)S(1)}, u32[]{:S(2)}, u32[]{:S(2)}) async-start(bf16[8,1,6,16,128]{4,3,2,1,0:T(8,128)(2,1)} %bitcast.80), calls=%async_computation | async-start | bytes 393216 | tf_op jit(solution)/shard_map/all_to_all | solution.py:461
